TPU v7x, 32 devices: a whole 2x2x4 slice. The times are simulated.
32 devices in a mesh: grp: 4 (over z), lane: 8 (over y, x, core).
Axes of the slice: x: 2, y: 2, z: 4, core: 2. Of those that a mesh axis runs over, the one named last changes fastest.
Arguments:
- factor_left: float32 [1048576], P(('grp', 'lane')), may hold values from -7 to 7, as said below
- denom_right: float32 [1048576], P(('grp', 'lane')), may hold values from -7 to 7, as said below
- bessel_left: float32 [1048576], P(('grp', 'lane')), may hold values from -7 to 7, as said below
- bessel_right: float32 [1048576], P(('grp', 'lane')), may hold values from -7 to 7, as said below
- harmonic_left: float32 [1048576], P(('grp', 'lane')), may hold values from -7 to 7, as said below
- harmonic_right: float32 [1048576], P(('grp', 'lane')), may hold values from -7 to 7, as said below
- weighted_left: float32 [1048576], P(('grp', 'lane')), may hold values from -7 to 7, as said below
Outputs:
- bessel_sum: float32 [2097152], P(('grp', 'lane'))
- harmonic_sum: float32 [2097152], P(('grp', 'lane'))
Inputs may be any that keep to these rules, and one draw needn't show every extreme that they name: `factor_left`: every limb is a whole number. `denom_right`: every limb is a whole number. `bessel_left`: every limb is a whole number. `bessel_right`: every limb is a whole number. `harmonic_left`: every limb is a whole number. `harmonic_right`: every limb is a whole number. `weighted_left`: every limb is a whole number.
All inputs are finite; a program needn't handle non-finite values.
Results may differ from a plain program's by a relative error of at most 0.00045.
Values sent between devices are 32-bit elements; how exact they have to be, the bound alone decides.
No kernel may reach another device: no remote copies, remote signals or barrier semaphores. Data moves between devices by JAX's collectives and lax.ppermute only.
A program may use at most 128 MiB of HBM per device.

v0:
```python
import math

import jax
import jax.numpy as jnp
import numpy as np
from jax import lax
from jax.experimental import pallas as pl
from jax.experimental.pallas import tpu as pltpu
from jax.sharding import PartitionSpec as P

AXES = ("grp", "lane")
LANES = 128
FWD_OPS = 7
VMEM = pltpu.MemorySpace.VMEM


def device_count():
    return lax.axis_size("grp") * lax.axis_size("lane")


def device_position():
    return lax.axis_index("grp") * lax.axis_size("lane") + lax.axis_index("lane")


def turn(numer, denom):
    reduced = numer % denom
    reduced = jnp.where(2 * reduced > denom, reduced - denom, reduced)
    angle = reduced.astype(jnp.float32) * (2.0 * math.pi / denom)
    return jnp.cos(angle), jnp.sin(angle)


def split16(value):
    high = value.astype(jnp.bfloat16)
    return high, (value - high.astype(jnp.float32)).astype(jnp.bfloat16)


def split_table(value):
    high = lax.reduce_precision(value, 8, 7)
    return high.astype(jnp.bfloat16), (value - high).astype(jnp.bfloat16)


def dot3(left, right):
    out = jnp.dot(left[0], right[1], preferred_element_type=jnp.float32)
    out += jnp.dot(left[1], right[0], preferred_element_type=jnp.float32)
    return out + jnp.dot(left[0], right[0], preferred_element_type=jnp.float32)


def tree_forward(values, numer, denom, emit):
    if len(values) == 1:
        emit(numer, denom, values[0])
        return
    half = len(values) // 2
    numer, denom = numer, 2 * denom
    cos, sin = math.cos(2 * math.pi * numer / denom), math.sin(2 * math.pi * numer / denom)
    plus, minus = [], []
    for low, high in zip(values[:half], values[half:]):
        if low[1] is None:
            re, im = cos * high[0], sin * high[0]
            plus.append((low[0] + re, im))
            minus.append((low[0] - re, -im))
        else:
            re = cos * high[0] - sin * high[1]
            im = sin * high[0] + cos * high[1]
            plus.append((low[0] + re, low[1] + im))
            minus.append((low[0] - re, low[1] - im))
    tree_forward(plus, numer, denom, emit)
    tree_forward(minus, numer + denom // 2, denom, emit)


def tree_inverse(size, numer, denom, load):
    if size == 1:
        return [load(numer, denom)]
    denom = 2 * denom
    cos, sin = math.cos(2 * math.pi * numer / denom), math.sin(2 * math.pi * numer / denom)
    plus = tree_inverse(size // 2, numer, denom, load)
    minus = tree_inverse(size // 2, numer + denom // 2, denom, load)
    low = [(a[0] + b[0], a[1] + b[1]) for a, b in zip(plus, minus)]
    high = []
    for a, b in zip(plus, minus):
        re, im = a[0] - b[0], a[1] - b[1]
        high.append((cos * re + sin * im, cos * im - sin * re))
    return low + high


def slot_of(numer, denom, devices):
    numer = (numer * (4 * devices // denom)) % (4 * devices)
    return (numer - 1) // 4


def spread_kernel(x_ref, out_ref):
    devices = x_ref.shape[0]

    def one(op, carry):
        values = [(x_ref[d, op], None) for d in range(devices)]

        def emit(numer, denom, value):
            slot = slot_of(numer, denom, devices)
            out_ref[slot, op, 0] = value[0]
            out_ref[slot, op, 1] = value[1]

        tree_forward(values, 1, 4, emit)
        return carry

    lax.fori_loop(0, x_ref.shape[1], one, 0)


def gather_kernel(u_ref, out_ref):
    devices = u_ref.shape[0]
    for out in range(u_ref.shape[1]):

        def load(numer, denom):
            slot = slot_of(numer, denom, devices)
            return u_ref[slot, out, 0], u_ref[slot, out, 1]

        for block, (re, im) in enumerate(tree_inverse(devices, 1, 4, load)):
            out_ref[block // 2, out, block % 2] = re
            out_ref[(devices + block) // 2, out, (devices + block) % 2] = im


def spectrum_kernel(x_ref, a_hi, a_lo, turn_ref, b_ref, h_ref, ai_hi, ai_lo, out_ref, spec_ref):
    rows = turn_ref.shape[1]
    turn_re, turn_im = turn_ref[0], turn_ref[1]
    table = (a_hi[...], a_lo[...])
    table_inv = (ai_hi[...], ai_lo[...])
    lane_table = (b_ref[0], b_ref[1])
    lane_table_inv = (b_ref[2], b_ref[3])

    def column_stage(stage_table, re, im):
        both = dot3(stage_table, split16(jnp.concatenate([re, im], axis=1)))
        top, bottom = both[:rows], both[rows:]
        return top[:, :LANES] - bottom[:, LANES:], top[:, LANES:] + bottom[:, :LANES]

    def forward(op, carry):
        re, im = column_stage(
            table, x_ref[:, op, 0].reshape(rows, LANES), x_ref[:, op, 1].reshape(rows, LANES)
        )
        turned = jnp.concatenate(
            [re * turn_re - im * turn_im, re * turn_im + im * turn_re], axis=1
        )
        spec_ref[op] = dot3(split16(turned), lane_table)
        return carry

    lax.fori_loop(0, FWD_OPS, forward, 0)

    def member(op):
        return spec_ref[op, :, :LANES], spec_ref[op, :, LANES:]

    def products(pairs):
        re, im = 0.0, 0.0
        for left, right in pairs:
            left_re, left_im = member(left)
            right_re, right_im = member(right)
            re = re + (left_re * right_re - left_im * right_im)
            im = im + (left_re * right_im + left_im * right_re)
        return re, im

    for out, pairs in enumerate((((2, 1), (0, 3)), ((4, 1), (0, 5), (6, 3)))):
        re, im = products(pairs)
        h_re, h_im = h_ref[0], h_ref[1]
        damped = jnp.concatenate([re * h_re - im * h_im, re * h_im + im * h_re], axis=1)
        both = dot3(split16(damped), lane_table_inv)
        re, im = both[:, :LANES], both[:, LANES:]
        re, im = re * turn_re + im * turn_im, im * turn_re - re * turn_im
        re, im = column_stage(table_inv, re, im)
        piece = (out_ref.shape[0],) + out_ref.shape[3:]
        out_ref[:, out, 0] = re.reshape(piece)
        out_ref[:, out, 1] = im.reshape(piece)


def call(kernel, out_shape, *args, scratch=()):
    return pl.pallas_call(
        kernel,
        out_shape=jax.ShapeDtypeStruct(out_shape, jnp.float32),
        in_specs=[pl.BlockSpec(memory_space=VMEM)] * len(args),
        out_specs=pl.BlockSpec(memory_space=VMEM),
        scratch_shapes=scratch,
    )(*args)


def exchange(value):
    return lax.all_to_all(value, AXES, split_axis=0, concat_axis=0, tiled=True)


def lane_tables():
    index = np.arange(LANES)
    angle = 2.0 * np.pi * ((index[:, None] * index[None, :]) % LANES) / LANES
    cos, sin = np.cos(angle), np.sin(angle)
    forward = np.block([[cos, sin], [-sin, cos]]).astype(np.float32)
    backward = np.block([[cos, -sin], [sin, cos]]).astype(np.float32)
    parts = []
    for table in (forward, backward):
        high = table.astype(jnp.bfloat16)
        parts += [high, (table - high.astype(np.float32)).astype(jnp.bfloat16)]
    return jnp.asarray(np.stack(parts))


def tables(local_limbs, devices, scaling, rate):
    rows = local_limbs // LANES
    period = 4 * local_limbs * devices
    freq = 4 * device_position() + 1

    def grid(shape):
        return (lax.broadcasted_iota(jnp.int32, shape, 0), lax.broadcasted_iota(jnp.int32, shape, 1))

    q1, t1 = grid((rows, rows))
    step = period // rows
    cos, sin = turn(((t1 * q1) % rows) * step + LANES * t1 * freq, period)
    forward = split_table(jnp.concatenate([cos, sin], axis=0))
    t1, q1 = grid((rows, rows))
    cos, sin = turn(((t1 * q1) % rows) * step + LANES * t1 * freq, period)
    backward = split_table(jnp.concatenate([cos, -sin], axis=0))
    q1, t2 = grid((rows, LANES))
    between = jnp.stack(turn(t2 * (q1 * (period // local_limbs) + freq), period))
    numer = freq + 4 * devices * (q1 + rows * t2)
    numer = jnp.where(2 * numer > period, numer - period, numer)
    angle = numer.astype(jnp.float32) * (2.0 * math.pi / period)
    half = jnp.sin(0.5 * angle)
    damp = math.exp(-rate)
    den_re = -math.expm1(-rate) + (2.0 * damp) * half * half
    den_im = -damp * jnp.sin(angle)
    norm = scaling / (den_re * den_re + den_im * den_im)
    filt = jnp.stack([den_re * norm, -den_im * norm])
    return forward, between, filt, backward


def damped_totals(stacked, rate, scaling):
    devices = device_count()
    local_limbs = stacked.shape[0] * stacked.shape[2] * LANES
    shape = (stacked.shape[0], 1, stacked.shape[2], LANES)
    index = (
        lax.broadcasted_iota(jnp.int32, shape, 0) * shape[2]
        + lax.broadcasted_iota(jnp.int32, shape, 2)
    ) * LANES + lax.broadcasted_iota(jnp.int32, shape, 3)
    left = (local_limbs - 1 - index) + (devices - 1 - device_position()) * local_limbs
    sums = jnp.sum(stacked * jnp.exp(left.astype(jnp.float32) * -rate), axis=(0, 2, 3))
    step = 1
    while step < devices:
        pairs = [(d, d ^ step) for d in range(devices)]
        sums = sums + lax.ppermute(sums, AXES, pairs)
        step *= 2
    factor = scaling * math.exp(-rate)
    return (
        factor * (sums[2] * sums[1] + sums[0] * sums[3]),
        factor * (sums[4] * sums[1] + sums[0] * sums[5] + sums[6] * sums[3]),
    )


def local(*operands):
    devices = device_count()
    local_limbs = operands[0].shape[0]
    total = local_limbs * devices
    rate = 1.0 / (2 * local_limbs)
    scaling = 1.0 / (16.0 * math.sqrt(total) * math.sqrt(local_limbs))
    rows = local_limbs // LANES
    piece = rows // devices
    inside = piece % 8 == 0

    stacked = jnp.stack([v.reshape(devices, piece, LANES) for v in operands], axis=1)
    received = exchange(stacked)
    ends = damped_totals(stacked, rate, scaling)
    forward, between, filt, backward = tables(local_limbs, devices, scaling / total, rate)

    spread = call(spread_kernel, (devices, FWD_OPS, 2, piece, LANES), received)
    landed = exchange(spread)
    if not inside:
        landed = landed.transpose(1, 2, 0, 3, 4).reshape(1, FWD_OPS, 2, rows, LANES)
    out_piece = (devices, 2, 2, piece, LANES) if inside else (1, 2, 2, rows, LANES)
    turned = call(
        spectrum_kernel,
        out_piece,
        landed,
        *forward,
        between,
        lane_tables(),
        filt,
        *backward,
        scratch=[pltpu.VMEM((FWD_OPS, rows, 2 * LANES), jnp.float32)],
    )
    if not inside:
        turned = turned.reshape(2, 2, devices, piece, LANES).transpose(2, 0, 1, 3, 4)
    gathered = exchange(turned)
    coeffs = call(gather_kernel, (devices, 2, 2, piece, LANES), gathered)
    owned = exchange(coeffs)

    results = []
    for out in range(2):
        mine = owned[:, out].transpose(1, 0, 2, 3).reshape(2 * local_limbs)
        index = lax.broadcasted_iota(jnp.int32, (2 * local_limbs,), 0)
        index = index + device_position() * (2 * local_limbs)
        decay = jnp.exp((index + 1).astype(jnp.float32) * -rate)
        results.append(mine + ends[out] * decay)
    return tuple(results)


def solution(mesh):
    return jax.shard_map(
        local,
        mesh=mesh,
        in_specs=(P(AXES),) * FWD_OPS,
        out_specs=(P(AXES), P(AXES)),
        check_vma=False,
    )
```

profile of v0, /device:TPU:0, one launch (start us, length us, event | category | flops | bytes accessed | tf_op | source)
XLA Modules:
  0.0 148.0 jit_solution(4806663361771347605)
XLA Ops:
  0.6 0.9 bitcast_dynamic-update-slice_fusion.6
  1.5 0.9 bitcast_dynamic-update-slice_fusion.5
  2.5 0.9 bitcast_dynamic-update-slice_fusion.4
  3.4 0.9 bitcast_dynamic-update-slice_fusion.3
  4.3 0.9 bitcast_dynamic-update-slice_fusion.2
  5.2 0.9 bitcast_dynamic-update-slice_fusion.1
  6.1 0.9 bitcast_dynamic-update-slice_fusion
  7.1 30.6 %all_to_all.20.x_ref = f32[32,7,8,128]{3,2,1,0:T(8,128)} all-to-all(f32[32,7,8,128]{3,2,1,0:T(8,128)S(1)} %bitcast_dynamic-update-slice_fusion), channel_id=1, replica_groups=mesh['grp'=4,'lane'=8] {'grp','lane'}, dimensions={0} | all-to-all | bytes 1835008 | tf_op jit(solution)/shard_map/all_to_all | solution.py:181
  37.7 3.2 %shard_map.95 = f32[32,7,2,8,128]{4,3,2,1,0:T(8,128)} custom-call(f32[32,7,8,128]{3,2,1,0:T(8,128)} %all_to_all.20.x_ref), custom_call_target="tpu_custom_call" | custom-call | tf_op jit(solution)/shard_map/pallas_call | solution.py:171
  40.9 3.6 %all-to-all-start.1 = ((f32[32,7,2,8,128]{4,3,2,1,0:T(8,128)}), f32[32,7,2,8,128]{4,3,2,1,0:T(8,128)S(1)}, u32[]{:S(2)}, u32[]{:S(2)}) async-start(f32[32,7,2,8,128]{4,3,2,1,0:T(8,128)} %shard_map.95), calls=%async_computation.1 | async-start | bytes 3670016 | tf_op jit(solution)/shard_map/all_to_all | solution.py:181
  44.6 1.0 fusion.18
  45.5 0.6 fusion.26
  46.2 0.8 pad_maximum_fusion.2
  47.0 2.3 %fusion.21 = (f32[256,256]{1,0:T(8,128)S(1)}, f32[256,256]{1,0:T(8,128)S(1)}, f32[256,256]{1,0:T(8,128)S(1)}, f32[256,256]{1,0:T(8,128)S(1)}) fusion(s32[256]{0:T(256)S(1)} %iota_multiply_fusion), kind=kLoop, calls=%fused_computation.68 | loop fusion | flops 3276800 | bytes 1049600 | tf_op jit(solution)/shard_map/cos | solution.py:29
  49.3 1.1 fusion
  50.4 37.3 %all-to-all-done.1.x_ref = f32[32,7,2,8,128]{4,3,2,1,0:T(8,128)S(1)} async-done(((f32[32,7,2,8,128]{4,3,2,1,0:T(8,128)}), f32[32,7,2,8,128]{4,3,2,1,0:T(8,128)S(1)}, u32[]{:S(2)}, u32[]{:S(2)}) %all-to-all-start.1) | async-done | bytes 1835040 | tf_op jit(solution)/shard_map/all_to_all | solution.py:181
  87.6 0.0 copy-start
  87.6 1.3 copy-done
  88.9 9.0 %shard_map.96 = f32[32,2,2,8,128]{4,3,2,1,0:T(8,128)} custom-call(f32[32,7,2,8,128]{4,3,2,1,0:T(8,128)} %copy-done, bf16[512,256]{1,0:T(8,128)(2,1)} %get-tuple-element.7.a_hi, bf16[512,256]{1,0:T(8,128)(2,1)} %get-tuple-element.6.a_lo, f32[2,256,128]{2,1,0:T(8,128)} %get-tuple-element.25.turn_ref, bf16[4,256,256]{2,1,0:T(8,128)(2,1)} %constant.108.clone.b_ref, ...), custom_call_target="tpu_custom_call" | custom-call | tf_op jit(solution)/shard_map/pallas_call | solution.py:171
  98.0 19.8 %all_to_all.21.u_ref = f32[32,2,2,8,128]{4,3,2,1,0:T(8,128)} all-to-all(f32[32,2,2,8,128]{4,3,2,1,0:T(8,128)} %shard_map.96), channel_id=1, replica_groups=mesh['grp'=4,'lane'=8] {'grp','lane'}, dimensions={0} | all-to-all | bytes 1048576 | tf_op jit(solution)/shard_map/all_to_all | solution.py:181
  117.8 2.1 %shard_map.97 = f32[32,2,2,8,128]{4,3,2,1,0:T(8,128)} custom-call(f32[32,2,2,8,128]{4,3,2,1,0:T(8,128)} %all_to_all.21.u_ref), custom_call_target="tpu_custom_call" | custom-call | tf_op jit(solution)/shard_map/pallas_call | solution.py:171
  119.9 3.0 %all-to-all-start.3 = ((f32[32,2,2,8,128]{4,3,2,1,0:T(8,128)}), f32[32,2,2,8,128]{4,3,2,1,0:T(8,128)S(1)}, u32[]{:S(2)}, u32[]{:S(2)}) async-start(f32[32,2,2,8,128]{4,3,2,1,0:T(8,128)} %shard_map.97), calls=%async_computation.3 | async-start | bytes 1048576 | tf_op jit(solution)/shard_map/all_to_all | solution.py:181
  122.9 0.1 multiply_exponential_fusion.1
  123.0 0.2 multiply_reduce_fusion
  123.2 0.3 collective-permute-start
  123.5 0.9 collective-permute-done
  124.4 1.8 %collective-permute-start.1 = (f32[7]{0:T(128)S(1)}, f32[7]{0:T(128)S(1)}, u32[]{:S(2)}, u32[]{:S(2)}) collective-permute-start(f32[7]{0:T(128)S(1)} %add.240), channel_id=1, source_target_pairs={{0,2},{1,3},{2,0},{3,1},{4,6},{5,7},{6,4},{7,5},{8,10},{9,11},{10,... | collective-permute-start | bytes 92 | tf_op jit(solution)/shard_map/ppermute | solution.py:239
  126.1 1.8 %collective-permute-done.1 = f32[7]{0:T(128)S(1)} collective-permute-done((f32[7]{0:T(128)S(1)}, f32[7]{0:T(128)S(1)}, u32[]{:S(2)}, u32[]{:S(2)}) %collective-permute-start.1) | collective-permute-done | bytes 60 | tf_op jit(solution)/shard_map/ppermute | solution.py:239
  128.0 2.0 %collective-permute-start.2 = (f32[7]{0:T(128)S(1)}, f32[7]{0:T(128)S(1)}, u32[]{:S(2)}, u32[]{:S(2)}) collective-permute-start(f32[7]{0:T(128)S(1)} %add.241), channel_id=1, source_target_pairs={{0,4},{1,5},{2,6},{3,7},{4,0},{5,1},{6,2},{7,3},{8,12},{9,13},{10,... | collective-permute-start | bytes 92 | tf_op jit(solution)/shard_map/ppermute | solution.py:239
  129.9 1.6 %collective-permute-done.2 = f32[7]{0:T(128)S(1)} collective-permute-done((f32[7]{0:T(128)S(1)}, f32[7]{0:T(128)S(1)}, u32[]{:S(2)}, u32[]{:S(2)}) %collective-permute-start.2) | collective-permute-done | bytes 60 | tf_op jit(solution)/shard_map/ppermute | solution.py:239
  131.5 1.8 %collective-permute-start.3 = (f32[7]{0:T(128)S(1)}, f32[7]{0:T(128)S(1)}, u32[]{:S(2)}, u32[]{:S(2)}) collective-permute-start(f32[7]{0:T(128)S(1)} %add.242), channel_id=1, source_target_pairs={{0,8},{1,9},{2,10},{3,11},{4,12},{5,13},{6,14},{7,15},{8,0},{9,1},... | collective-permute-start | bytes 92 | tf_op jit(solution)/shard_map/ppermute | solution.py:239
  133.3 1.8 %collective-permute-done.3 = f32[7]{0:T(128)S(1)} collective-permute-done((f32[7]{0:T(128)S(1)}, f32[7]{0:T(128)S(1)}, u32[]{:S(2)}, u32[]{:S(2)}) %collective-permute-start.3) | collective-permute-done | bytes 60 | tf_op jit(solution)/shard_map/ppermute | solution.py:239
  135.1 2.7 %collective-permute-start.4 = (f32[7]{0:T(128)S(1)}, f32[7]{0:T(128)S(1)}, u32[]{:S(2)}, u32[]{:S(2)}) collective-permute-start(f32[7]{0:T(128)S(1)} %add.243), channel_id=1, source_target_pairs={{0,16},{1,17},{2,18},{3,19},{4,20},{5,21},{6,22},{7,23},{8,24},{9,... | collective-permute-start | bytes 92 | tf_op jit(solution)/shard_map/ppermute | solution.py:239
  137.8 1.8 %collective-permute-done.4 = f32[7]{0:T(128)S(1)} collective-permute-done((f32[7]{0:T(128)S(1)}, f32[7]{0:T(128)S(1)}, u32[]{:S(2)}, u32[]{:S(2)}) %collective-permute-start.4) | collective-permute-done | bytes 60 | tf_op jit(solution)/shard_map/ppermute | solution.py:239
  139.6 0.7 fusion.27
  146.3 0.0 all-to-all-done.3
  146.5 0.8 multiply_add_fusion
  147.2 0.8 multiply_add_fusion.1
  (12 shorter events, 0.1 us)
Async XLA Ops:
  40.9 46.7 %all-to-all-start.1 = ((f32[32,7,2,8,128]{4,3,2,1,0:T(8,128)}), f32[32,7,2,8,128]{4,3,2,1,0:T(8,128)S(1)}, u32[]{:S(2)}, u32[]{:S(2)}) async-start(f32[32,7,2,8,128]{4,3,2,1,0:T(8,128)} %shard_map.95), calls=%async_computation.1 | async-start | bytes 3670016 | tf_op jit(solution)/shard_map/all_to_all | solution.py:181
  87.6 1.3 copy-start
  119.9 26.5 %all-to-all-start.3 = ((f32[32,2,2,8,128]{4,3,2,1,0:T(8,128)}), f32[32,2,2,8,128]{4,3,2,1,0:T(8,128)S(1)}, u32[]{:S(2)}, u32[]{:S(2)}) async-start(f32[32,2,2,8,128]{4,3,2,1,0:T(8,128)} %shard_map.97), calls=%async_computation.3 | async-start | bytes 1048576 | tf_op jit(solution)/shard_map/all_to_all | solution.py:181
  123.2 1.2 collective-permute-start
  124.4 3.6 %collective-permute-start.1 = (f32[7]{0:T(128)S(1)}, f32[7]{0:T(128)S(1)}, u32[]{:S(2)}, u32[]{:S(2)}) collective-permute-start(f32[7]{0:T(128)S(1)} %add.240), channel_id=1, source_target_pairs={{0,2},{1,3},{2,0},{3,1},{4,6},{5,7},{6,4},{7,5},{8,10},{9,11},{10,... | collective-permute-start | bytes 92 | tf_op jit(solution)/shard_map/ppermute | solution.py:239
  128.0 3.6 %collective-permute-start.2 = (f32[7]{0:T(128)S(1)}, f32[7]{0:T(128)S(1)}, u32[]{:S(2)}, u32[]{:S(2)}) collective-permute-start(f32[7]{0:T(128)S(1)} %add.241), channel_id=1, source_target_pairs={{0,4},{1,5},{2,6},{3,7},{4,0},{5,1},{6,2},{7,3},{8,12},{9,13},{10,... | collective-permute-start | bytes 92 | tf_op jit(solution)/shard_map/ppermute | solution.py:239
  131.5 3.6 %collective-permute-start.3 = (f32[7]{0:T(128)S(1)}, f32[7]{0:T(128)S(1)}, u32[]{:S(2)}, u32[]{:S(2)}) collective-permute-start(f32[7]{0:T(128)S(1)} %add.242), channel_id=1, source_target_pairs={{0,8},{1,9},{2,10},{3,11},{4,12},{5,13},{6,14},{7,15},{8,0},{9,1},... | collective-permute-start | bytes 92 | tf_op jit(solution)/shard_map/ppermute | solution.py:239
  135.1 4.5 %collective-permute-start.4 = (f32[7]{0:T(128)S(1)}, f32[7]{0:T(128)S(1)}, u32[]{:S(2)}, u32[]{:S(2)}) collective-permute-start(f32[7]{0:T(128)S(1)} %add.243), channel_id=1, source_target_pairs={{0,16},{1,17},{2,18},{3,19},{4,20},{5,21},{6,22},{7,23},{8,24},{9,... | collective-permute-start | bytes 92 | tf_op jit(solution)/shard_map/ppermute | solution.py:239
where the time goes:
time: 149 us; the launch traced here: 148 us
  blocking collectives  50.5 us (34%)
  waiting for transfers between devices  45.2 us (30%)
  starting transfers between devices  15.1 us (10%)
  Pallas kernels  14.3 us (10%)
  local copies, waits for them, and re-layouts  8.44 us (6%)
  other arithmetic  7.65 us (5%)
  between operations  6.87 us (5%)
    all_to_all x2, blocking collectives, exchange(): return lax.all_to_all(value, AXES, split_axis=0, concat_axis=0, tiled=True)  50.5 us
    all_to_all x2, waiting for transfers between devices, exchange(): return lax.all_to_all(value, AXES, split_axis=0, concat_axis=0, tiled=True)  37.3 us
    pallas_call x3, Pallas kernels, call(): pl.pallas_call(kernel, out_shape=jax.ShapeDtypeStruct(out_shape, jnp.floa...  14.3 us
    ppermute x5, starting transfers between devices, damped_totals(): sums = sums + lax.ppermute(sums, AXES, pairs)  8.51 us
    ppermute x5, waiting for transfers between devices, damped_totals(): sums = sums + lax.ppermute(sums, AXES, pairs)  7.87 us
    unnamed x8, local copies, waits for them, and re-layouts  6.77 us
    all_to_all x2, starting transfers between devices, exchange(): return lax.all_to_all(value, AXES, split_axis=0, concat_axis=0, tiled=True)  6.59 us
  transfers between devices with their start and end apart: 7, of which 6 were waited for; matrix products, arithmetic and copies ran while one was open for 5% of the time, Pallas kernels for 0%

commit v1 on v0

v1 whole, which is shorter than its diff:
```python
import math

import jax
import jax.numpy as jnp
import numpy as np
from jax import lax
from jax.experimental import pallas as pl
from jax.experimental.pallas import tpu as pltpu
from jax.sharding import PartitionSpec as P

AXES = ("grp", "lane")
LANES = 128
FWD_OPS = 7
CARRY_ROWS = 4
VMEM = pltpu.MemorySpace.VMEM


def device_count():
    return lax.axis_size("grp") * lax.axis_size("lane")


def device_position():
    return lax.axis_index("grp") * lax.axis_size("lane") + lax.axis_index("lane")


def turn(numer, denom):
    reduced = numer % denom
    reduced = jnp.where(2 * reduced > denom, reduced - denom, reduced)
    angle = reduced.astype(jnp.float32) * (2.0 * math.pi / denom)
    return jnp.cos(angle), jnp.sin(angle)


def split16(value):
    high = value.astype(jnp.bfloat16)
    return high, (value - high.astype(jnp.float32)).astype(jnp.bfloat16)


def split_table(value):
    high = lax.reduce_precision(value, 8, 7)
    return high.astype(jnp.bfloat16), (value - high).astype(jnp.bfloat16)


def wide_left(parts):
    return jnp.concatenate([parts[0], parts[1], parts[0]], axis=1)


def tall_right(parts):
    return jnp.concatenate([parts[0], parts[0], parts[1]], axis=0)


def dot32(left, right):
    return jnp.dot(left, right, preferred_element_type=jnp.float32)


def tree_forward(values, numer, denom, emit):
    if len(values) == 1:
        emit(numer, denom, values[0])
        return
    half = len(values) // 2
    numer, denom = numer, 2 * denom
    cos, sin = math.cos(2 * math.pi * numer / denom), math.sin(2 * math.pi * numer / denom)
    plus, minus = [], []
    for low, high in zip(values[:half], values[half:]):
        if low[1] is None:
            re, im = cos * high[0], sin * high[0]
            plus.append((low[0] + re, im))
            minus.append((low[0] - re, -im))
        else:
            re = cos * high[0] - sin * high[1]
            im = sin * high[0] + cos * high[1]
            plus.append((low[0] + re, low[1] + im))
            minus.append((low[0] - re, low[1] - im))
    tree_forward(plus, numer, denom, emit)
    tree_forward(minus, numer + denom // 2, denom, emit)


def tree_inverse(size, numer, denom, load):
    if size == 1:
        return [load(numer, denom)]
    denom = 2 * denom
    cos, sin = math.cos(2 * math.pi * numer / denom), math.sin(2 * math.pi * numer / denom)
    plus = tree_inverse(size // 2, numer, denom, load)
    minus = tree_inverse(size // 2, numer + denom // 2, denom, load)
    low = [(a[0] + b[0], a[1] + b[1]) for a, b in zip(plus, minus)]
    high = []
    for a, b in zip(plus, minus):
        re, im = a[0] - b[0], a[1] - b[1]
        high.append((cos * re + sin * im, cos * im - sin * re))
    return low + high


def slot_of(numer, denom, devices):
    numer = (numer * (4 * devices // denom)) % (4 * devices)
    return (numer - 1) // 4


def spread_kernel(x_ref, out_far, out_ref, sems):
    devices = x_ref.shape[0]
    copies = []
    for op in range(FWD_OPS):
        values = [(x_ref[d, op], None) for d in range(devices)]

        def emit(numer, denom, value):
            slot = slot_of(numer, denom, devices)
            out_ref[op, slot, 0] = value[0]
            out_ref[op, slot, 1] = value[1]

        tree_forward(values, 1, 4, emit)
        copies.append(pltpu.make_async_copy(out_ref.at[op], out_far.at[:, op], sems.at[op]))
        copies[-1].start()
    for copy in copies:
        copy.wait()


def gather_kernel(u_ref, last_ref, decay_ref, out_ref):
    devices = u_ref.shape[0]
    rows = decay_ref.shape[0]
    packed = len(u_ref.shape) == 4
    for out in range(2):

        def part(slot, which):
            if not packed:
                return u_ref[slot, out, which]
            groups = rows // CARRY_ROWS
            first = (2 * out + which) * groups
            return jnp.concatenate([u_ref[slot, first + k] for k in range(groups)], axis=0)

        def last(slot, which):
            row = 2 * out + which
            ref = u_ref.at[slot, u_ref.shape[1] - 1] if packed else last_ref.at[slot]
            return ref[row : row + 1]

        wrap = 0.0
        for slot in range(devices):
            angle = 2.0 * math.pi * ((devices - 1) * (4 * slot + 1)) / (4 * devices)
            wrap = wrap + (math.cos(angle) * last(slot, 1) - math.sin(angle) * last(slot, 0))
        lane = lax.broadcasted_iota(jnp.int32, wrap.shape, 1)
        wrap = jnp.sum(jnp.where(lane == LANES - 1, wrap, 0.0), axis=1, keepdims=True)
        tail = decay_ref[...] * wrap

        def load(numer, denom):
            slot = slot_of(numer, denom, devices)
            return part(slot, 0), part(slot, 1)

        for block, pair in enumerate(tree_inverse(devices, 1, 4, load)):
            for k, value in enumerate(pair):
                index = k * devices + block
                value = value + math.exp(-0.5 * index) * tail
                out_ref[index // 2, out, index % 2] = value


def copy_all(pairs, sems):
    copies = [pltpu.make_async_copy(a, b, sems.at[k]) for k, (a, b) in enumerate(pairs)]
    for copy in copies:
        copy.start()
    return copies


def stack_kernel(*refs):
    operands, out_ref, sems = refs[:-2], refs[-2], refs[-1]
    pairs = [(ref, out_ref.at[:, op]) for op, ref in enumerate(operands)]
    for copy in copy_all(pairs, sems):
        copy.wait()


def deliver_kernel(in_ref, first_ref, second_ref, sems):
    pairs = [
        (in_ref.at[:, out, half], ref.at[half])
        for out, ref in enumerate((first_ref, second_ref))
        for half in range(2)
    ]
    for copy in copy_all(pairs, sems):
        copy.wait()


def spectrum_kernel(
    x_ref, a_ref, turn_ref, b_ref, h_far, ai_far, out_ref, spec_ref, h_ref, ai_ref, sems
):
    rows = turn_ref.shape[1]
    copies = copy_all([(h_far, h_ref), (ai_far, ai_ref)], sems)

    def column_stage(table_ref, re, im):
        both = dot32(table_ref[...], tall_right(split16(jnp.concatenate([re, im], axis=1))))
        top, bottom = both[:rows], both[rows:]
        return top[:, :LANES] - bottom[:, LANES:], top[:, LANES:] + bottom[:, :LANES]

    for op in range(FWD_OPS):
        re, im = column_stage(
            a_ref, x_ref[:, op, 0].reshape(rows, LANES), x_ref[:, op, 1].reshape(rows, LANES)
        )
        turn_re, turn_im = turn_ref[0], turn_ref[1]
        turned = jnp.concatenate(
            [re * turn_re - im * turn_im, re * turn_im + im * turn_re], axis=1
        )
        spec_ref[op] = dot32(wide_left(split16(turned)), b_ref[0])

    for copy in copies:
        copy.wait()

    def store(out, which, value):
        if len(out_ref.shape) == 5:
            out_ref[:, out, which] = value.reshape((out_ref.shape[0],) + out_ref.shape[3:])
            return
        devices = out_ref.shape[0]
        groups = rows // devices // CARRY_ROWS
        value = value.reshape(devices, groups * CARRY_ROWS, LANES)
        for k in range(groups):
            part = value[:, k * CARRY_ROWS : (k + 1) * CARRY_ROWS]
            out_ref[:, (2 * out + which) * groups + k] = part
        row = value[devices - 1 :, groups * CARRY_ROWS - 1 :]
        out_ref[:, 4 * groups, pl.ds(2 * out + which, 1)] = jnp.broadcast_to(
            row, (devices, 1, LANES)
        ).reshape(devices, 1, LANES)

    def member(op):
        return spec_ref[op, :, :LANES], spec_ref[op, :, LANES:]

    def products(pairs):
        re, im = 0.0, 0.0
        for left, right in pairs:
            left_re, left_im = member(left)
            right_re, right_im = member(right)
            re = re + (left_re * right_re - left_im * right_im)
            im = im + (left_re * right_im + left_im * right_re)
        return re, im

    for out, pairs in enumerate((((2, 1), (0, 3)), ((4, 1), (0, 5), (6, 3)))):
        re, im = products(pairs)
        h_re, h_im = h_ref[0], h_ref[1]
        damped = jnp.concatenate([re * h_re - im * h_im, re * h_im + im * h_re], axis=1)
        both = dot32(wide_left(split16(damped)), b_ref[1])
        re, im = both[:, :LANES], both[:, LANES:]
        turn_re, turn_im = turn_ref[0], turn_ref[1]
        re, im = re * turn_re + im * turn_im, im * turn_re - re * turn_im
        re, im = column_stage(ai_ref, re, im)
        for which, value in enumerate((re, im)):
            store(out, which, value)


def call(kernel, name, out_shapes, *args, near, scratch=()):
    spaces = [VMEM if flag else pltpu.MemorySpace.HBM for flag in near]
    args = [pltpu.with_memory_space_constraint(v, space) for v, space in zip(args, spaces)]
    specs = [pl.BlockSpec(memory_space=space) for space in spaces]
    outs = [space(shape, jnp.float32) for shape, space in zip(out_shapes, spaces[len(args) :])]
    return pl.pallas_call(
        kernel,
        out_shape=outs,
        in_specs=specs[: len(args)],
        out_specs=specs[len(args) :],
        scratch_shapes=scratch,
        compiler_params=pltpu.CompilerParams(vmem_limit_bytes=24 << 20),
        name=name,
    )(*args)


def exchange(value):
    return lax.all_to_all(value, AXES, split_axis=0, concat_axis=0, tiled=True)


def lane_tables():
    index = np.arange(LANES)
    angle = 2.0 * np.pi * ((index[:, None] * index[None, :]) % LANES) / LANES
    cos, sin = np.cos(angle), np.sin(angle)
    forward = np.block([[cos, sin], [-sin, cos]]).astype(np.float32)
    backward = np.block([[cos, -sin], [sin, cos]]).astype(np.float32)
    parts = []
    for table in (forward, backward):
        high = table.astype(jnp.bfloat16)
        low = (table - high.astype(np.float32)).astype(jnp.bfloat16)
        parts.append(np.concatenate([high, high, low], axis=0))
    return jnp.asarray(np.stack(parts))


def tables(local_limbs, devices, scaling, rate):
    rows = local_limbs // LANES
    period = 4 * local_limbs * devices
    freq = 4 * device_position() + 1

    def grid(shape):
        return (lax.broadcasted_iota(jnp.int32, shape, 0), lax.broadcasted_iota(jnp.int32, shape, 1))

    q1, t1 = grid((rows, rows))
    step = period // rows
    cos, sin = turn(((t1 * q1) % rows) * step + LANES * t1 * freq, period)
    forward = wide_left(split_table(jnp.concatenate([cos, sin], axis=0)))
    t1, q1 = grid((rows, rows))
    cos, sin = turn(((t1 * q1) % rows) * step + LANES * t1 * freq, period)
    backward = wide_left(split_table(jnp.concatenate([cos, -sin], axis=0)))
    q1, t2 = grid((rows, LANES))
    between = jnp.stack(turn(t2 * (q1 * (period // local_limbs) + freq), period))
    numer = freq + 4 * devices * (q1 + rows * t2)
    numer = jnp.where(2 * numer > period, numer - period, numer)
    angle = numer.astype(jnp.float32) * (2.0 * math.pi / period)
    half = jnp.sin(0.5 * angle)
    damp = math.exp(-rate)
    den_re = -math.expm1(-rate) + (2.0 * damp) * half * half
    den_im = -damp * jnp.sin(angle)
    norm = scaling / (den_re * den_re + den_im * den_im)
    filt = jnp.stack([den_re * norm, -den_im * norm])
    return forward, between, filt, backward


def local(*operands):
    devices = device_count()
    local_limbs = operands[0].shape[0]
    total = local_limbs * devices
    rate = 1.0 / (2 * local_limbs)
    scaling = 1.0 / (16.0 * math.sqrt(total) * math.sqrt(local_limbs))
    rows = local_limbs // LANES
    piece = rows // devices
    inside = piece % 8 == 0

    dma = pltpu.SemaphoreType.DMA
    far_ops = [v.reshape(devices, piece, LANES) for v in operands]
    (stacked,) = call(
        stack_kernel,
        "stack",
        [(devices, FWD_OPS, piece, LANES)],
        *far_ops,
        near=[False] * FWD_OPS + [True],
        scratch=[dma((FWD_OPS,))],
    )
    received = exchange(stacked)
    forward, between, filt, backward = tables(local_limbs, devices, scaling / total, rate)
    consts = (forward, between, lane_tables(), filt, backward)
    shape = (piece, LANES)
    index = (device_position() * piece + lax.broadcasted_iota(jnp.int32, shape, 0)) * LANES
    index = index + lax.broadcasted_iota(jnp.int32, shape, 1)
    decay = jnp.exp((index + 1).astype(jnp.float32) * -rate)

    (spread,) = call(
        spread_kernel,
        "spread",
        [(devices, FWD_OPS, 2, piece, LANES)],
        received,
        near=[True, False],
        scratch=[
            pltpu.VMEM((FWD_OPS, devices, 2, piece, LANES), jnp.float32),
            dma((FWD_OPS,)),
        ],
    )
    landed = exchange(spread)
    if not inside:
        landed = landed.transpose(1, 2, 0, 3, 4).reshape(1, FWD_OPS, 2, rows, LANES)
    groups = 4 * piece // CARRY_ROWS
    packed = (devices, groups + 1, CARRY_ROWS, LANES)
    (turned,) = call(
        spectrum_kernel,
        "spectrum",
        [packed if inside else (1, 2, 2, rows, LANES)],
        landed,
        *consts,
        near=[True] * 4 + [False] * 2 + [True],
        scratch=[
            pltpu.VMEM((FWD_OPS, rows, 2 * LANES), jnp.float32),
            pltpu.VMEM(filt.shape, filt.dtype),
            pltpu.VMEM(backward.shape, backward.dtype),
            dma((2,)),
        ],
    )
    if not inside:
        data = turned.reshape(4, devices, piece, LANES).transpose(1, 0, 2, 3)
        last = jnp.broadcast_to(turned[0, :, :, -1].reshape(1, 1, 4, LANES), (devices, 1, 4, LANES))
        turned = jnp.concatenate([data.reshape(devices, groups, CARRY_ROWS, LANES), last], axis=1)
    gathered = exchange(turned)
    last = gathered[:, groups] if not inside else decay
    if not inside:
        gathered = gathered[:, :groups].reshape(devices, 2, 2, piece, LANES)
    (coeffs,) = call(
        gather_kernel,
        "gather",
        [(devices, 2, 2, piece, LANES)],
        gathered,
        last,
        decay,
        near=[True] * 4,
    )
    owned = exchange(coeffs)
    results = call(
        deliver_kernel,
        "deliver",
        [(2, devices, piece, LANES)] * 2,
        owned,
        near=[True, False, False],
        scratch=[dma((4,))],
    )
    return tuple(v.reshape(2 * local_limbs) for v in results)


def solution(mesh):
    return jax.shard_map(
        local,
        mesh=mesh,
        in_specs=(P(AXES),) * FWD_OPS,
        out_specs=(P(AXES), P(AXES)),
        check_vma=False,
    )
```

time: 149 us -> 130 us (0.87)
  waiting for transfers between devices: 45.2 us -> 54 us
  starting transfers between devices: 15.1 us -> 7.75 us
  local copies, waits for them, and re-layouts: 8.44 us -> 1.13 us
  between operations: 6.87 us -> 0.75 us
  Pallas kernels: 14.3 us -> 10.7 us
  other arithmetic: 7.65 us -> 5.84 us
    all_to_all x2, waiting for transfers between devices: 37.3 us -> 54 us  [exchange(): return lax.all_to_all(value, AXES, split_axis=0, concat_axis=0, tiled=True)]
    ppermute x5 -> x0, starting transfers between devices: 8.51 us -> none  [damped_totals(): sums = sums + lax.ppermute(sums, AXES, pairs)]
    ppermute x5 -> x0, waiting for transfers between devices: 7.87 us -> none  [damped_totals(): sums = sums + lax.ppermute(sums, AXES, pairs)]
    unnamed x8 -> x2, local copies, waits for them, and re-layouts: 6.77 us -> 1.13 us
    pallas_call x3 -> x5, Pallas kernels: 14.3 us -> 10.7 us  [call(): pl.pallas_call(kernel, out_shape=outs, in_specs=specs[:len(args)], out_sp...]
    add x7 -> x0, other arithmetic: 1.59 us -> none  [the longest x2 1.58 us: local(): results.append(mine + ends[out] * decay)]
  transfers between devices with their start and end apart: 7 -> 2, of which waited for: 6 -> 2; matrix products, arithmetic and copies ran while one was open for 5% -> 5% of each run, Pallas kernels for 0% -> 0%
where the time goes in v1:
time: 130 us; the launch traced here: 129 us
  waiting for transfers between devices  54 us (42%)
  blocking collectives  49.1 us (38%)
  Pallas kernels  10.7 us (8%)
  starting transfers between devices  7.75 us (6%)
  other arithmetic  5.84 us (4%)
    all_to_all x2, waiting for transfers between devices, exchange(): return lax.all_to_all(value, AXES, split_axis=0, concat_axis=0, tiled=True)  54 us
    all_to_all x2, blocking collectives, exchange(): return lax.all_to_all(value, AXES, split_axis=0, concat_axis=0, tiled=True)  49.1 us
    pallas_call x5, Pallas kernels, call(): pl.pallas_call(kernel, out_shape=outs, in_specs=specs[:len(args)], out_sp...  10.7 us
    all_to_all x2, starting transfers between devices, exchange(): return lax.all_to_all(value, AXES, split_axis=0, concat_axis=0, tiled=True)  7.75 us
    cos x2, other arithmetic, turn(): return (jnp.cos(angle), jnp.sin(angle))  2.9 us
  transfers between devices with their start and end apart: 2, of which 2 were waited for; matrix products, arithmetic and copies ran while one was open for 5% of the time, Pallas kernels for 0%

profile of v1, /device:TPU:0, one launch (start us, length us, event | category | flops | bytes accessed | tf_op | source)
XLA Modules:
  0.0 129.2 jit_solution(11031126159838135574)
XLA Ops:
  0.6 1.3 %stack.13 = f32[32,7,8,128]{3,2,1,0:T(8,128)S(1)} custom-call(f32[32,8,128]{2,1,0:T(8,128)} %bitcast.9, f32[32,8,128]{2,1,0:T(8,128)} %bitcast.10, f32[32,8,128]{2,1,0:T(8,128)} %bitcast.11, f32[32,8,128]{2,1,0:T(8,128)} %bitcast.12, f32[32,8,128]{2,1,0:T(8,128)} %bitcast.13, f32[32,8,128]{2,1,0:T(8,128)} %bitcast.14, f32[32,8,128]{2,1,0:T(8,128)} %bitcast.15), custom_call_target="tpu_custom_call" | custom-call | tf_op jit(solution)/shard_map/stack/pallas_call | solution.py:245
  1.9 30.5 %all_to_all.20.x_ref = f32[32,7,8,128]{3,2,1,0:T(8,128)S(1)} all-to-all(f32[32,7,8,128]{3,2,1,0:T(8,128)S(1)} %stack.13), channel_id=1, replica_groups=mesh['grp'=4,'lane'=8] {'grp','lane'}, dimensions={0} | all-to-all | bytes 1835008 | tf_op jit(solution)/shard_map/all_to_all | solution.py:257
  32.5 1.6 %spread.1 = f32[32,7,2,8,128]{4,3,2,1,0:T(8,128)} custom-call(f32[32,7,8,128]{3,2,1,0:T(8,128)S(1)} %all_to_all.20.x_ref), custom_call_target="tpu_custom_call" | custom-call | tf_op jit(solution)/shard_map/spread/pallas_call | solution.py:245
  34.0 3.6 %all-to-all-start.1 = ((f32[32,7,2,8,128]{4,3,2,1,0:T(8,128)}), f32[32,7,2,8,128]{4,3,2,1,0:T(8,128)S(1)}, u32[]{:S(2)}, u32[]{:S(2)}) async-start(f32[32,7,2,8,128]{4,3,2,1,0:T(8,128)} %spread.1), calls=%async_computation.1 | async-start | bytes 3670016 | tf_op jit(solution)/shard_map/all_to_all | solution.py:257
  37.7 1.0 fusion.18
  38.7 0.6 fusion.26
  39.3 0.7 pad_maximum_fusion.4
  40.0 2.3 %fusion.21 = (f32[256,256]{1,0:T(8,128)S(1)}, f32[256,256]{1,0:T(8,128)S(1)}, f32[256,256]{1,0:T(8,128)S(1)}, f32[256,256]{1,0:T(8,128)S(1)}) fusion(s32[256]{0:T(256)S(1)} %iota_multiply_fusion), kind=kLoop, calls=%fused_computation.56 | loop fusion | flops 3276800 | bytes 1049600 | tf_op jit(solution)/shard_map/cos | solution.py:30
  42.3 0.2 fusion
  42.5 0.1 pad_maximum_fusion.a_ref
  42.5 0.9 pad_maximum_fusion.1.ai_far
  43.5 37.3 %all-to-all-done.1.x_ref = f32[32,7,2,8,128]{4,3,2,1,0:T(8,128)S(1)} async-done(((f32[32,7,2,8,128]{4,3,2,1,0:T(8,128)}), f32[32,7,2,8,128]{4,3,2,1,0:T(8,128)S(1)}, u32[]{:S(2)}, u32[]{:S(2)}) %all-to-all-start.1) | async-done | bytes 1835040 | tf_op jit(solution)/shard_map/all_to_all | solution.py:257
  80.8 0.0 copy-start
  80.8 1.1 copy-done
  81.9 6.6 %spectrum.1 = f32[32,9,4,128]{3,2,1,0:T(4,128)} custom-call(f32[32,7,2,8,128]{4,3,2,1,0:T(8,128)S(1)} %all-to-all-done.1.x_ref, bf16[512,768]{1,0:T(8,128)(2,1)S(1)} %pad_maximum_fusion.a_ref, f32[2,256,128]{2,1,0:T(8,128)S(1)} %get-tuple-element.20.turn_ref, bf16[2,768,256]{2,1,0:T(8,128)(2,1)S(1)} %copy-done, f32[2,256,128]{2,1,0:T(8,128)} %get-tuple-element.21.h_far, ...), custom_call_target="tpu_custom_call" | custom-call | tf_op jit(solution)/shard_map/spectrum/pallas_call | solution.py:245
  88.5 4.1 %all-to-all-start.2 = ((f32[32,9,4,128]{3,2,1,0:T(4,128)}), f32[32,9,4,128]{3,2,1,0:T(4,128)S(1)}, u32[]{:S(2)}, u32[]{:S(2)}) async-start(f32[32,9,4,128]{3,2,1,0:T(4,128)} %spectrum.1), calls=%async_computation.2 | async-start | bytes 1179648 | tf_op jit(solution)/shard_map/all_to_all | solution.py:257
  92.7 0.1 multiply_exponential_fusion.last_ref.decay_ref
  92.8 16.7 %all-to-all-done.2.u_ref = f32[32,9,4,128]{3,2,1,0:T(4,128)S(1)} async-done(((f32[32,9,4,128]{3,2,1,0:T(4,128)}), f32[32,9,4,128]{3,2,1,0:T(4,128)S(1)}, u32[]{:S(2)}, u32[]{:S(2)}) %all-to-all-start.2) | async-done | bytes 589856 | tf_op jit(solution)/shard_map/all_to_all | solution.py:257
  109.5 0.3 gather.1
  109.8 18.6 %all_to_all.21.in_ref = f32[32,2,2,8,128]{4,3,2,1,0:T(8,128)S(1)} all-to-all(f32[32,2,2,8,128]{4,3,2,1,0:T(8,128)S(1)} %gather.1), channel_id=1, replica_groups=mesh['grp'=4,'lane'=8] {'grp','lane'}, dimensions={0} | all-to-all | bytes 1048576 | tf_op jit(solution)/shard_map/all_to_all | solution.py:257
  128.4 0.8 deliver.1
  (4 shorter events, 0.0 us)
Async XLA Ops:
  34.0 46.7 %all-to-all-start.1 = ((f32[32,7,2,8,128]{4,3,2,1,0:T(8,128)}), f32[32,7,2,8,128]{4,3,2,1,0:T(8,128)S(1)}, u32[]{:S(2)}, u32[]{:S(2)}) async-start(f32[32,7,2,8,128]{4,3,2,1,0:T(8,128)} %spread.1), calls=%async_computation.1 | async-start | bytes 3670016 | tf_op jit(solution)/shard_map/all_to_all | solution.py:257
  80.8 1.1 copy-start
  88.5 20.9 %all-to-all-start.2 = ((f32[32,9,4,128]{3,2,1,0:T(4,128)}), f32[32,9,4,128]{3,2,1,0:T(4,128)S(1)}, u32[]{:S(2)}, u32[]{:S(2)}) async-start(f32[32,9,4,128]{3,2,1,0:T(4,128)} %spectrum.1), calls=%async_computation.2 | async-start | bytes 1179648 | tf_op jit(solution)/shard_map/all_to_all | solution.py:257

commit v2 on v1

--- a/solution.py
+++ b/solution.py
@@ -174,10 +174,11 @@
 
 
 def spectrum_kernel(
-    x_ref, a_ref, turn_ref, b_ref, h_far, ai_far, out_ref, spec_ref, h_ref, ai_ref, sems
+    x_ref, a_ref, turn_ref, b_far, h_far, ai_far, out_ref,
+    spec_ref, lhs_ref, b_ref, h_ref, ai_ref, sems,
 ):
     rows = turn_ref.shape[1]
-    copies = copy_all([(h_far, h_ref), (ai_far, ai_ref)], sems)
+    copies = copy_all([(b_far, b_ref), (h_far, h_ref), (ai_far, ai_ref)], sems)
 
     def column_stage(table_ref, re, im):
         both = dot32(table_ref[...], tall_right(split16(jnp.concatenate([re, im], axis=1))))
@@ -192,10 +193,13 @@
         turned = jnp.concatenate(
             [re * turn_re - im * turn_im, re * turn_im + im * turn_re], axis=1
         )
-        spec_ref[op] = dot32(wide_left(split16(turned)), b_ref[0])
+        lhs_ref[op] = wide_left(split16(turned))
 
     for copy in copies:
         copy.wait()
+    shape = spec_ref.shape
+    left = lhs_ref[...].reshape(shape[0] * shape[1], lhs_ref.shape[2])
+    spec_ref[...] = dot32(left, b_ref[0]).reshape(shape)
 
     def store(out, which, value):
         if len(out_ref.shape) == 5:
@@ -350,13 +354,13 @@
         [packed if inside else (1, 2, 2, rows, LANES)],
         landed,
         *consts,
-        near=[True] * 4 + [False] * 2 + [True],
+        near=[True] * 3 + [False] * 3 + [True],
         scratch=[
             pltpu.VMEM((FWD_OPS, rows, 2 * LANES), jnp.float32),
-            pltpu.VMEM(filt.shape, filt.dtype),
-            pltpu.VMEM(backward.shape, backward.dtype),
-            dma((2,)),
-        ],
+            pltpu.VMEM((FWD_OPS, rows, 6 * LANES), jnp.bfloat16),
+        ]
+        + [pltpu.VMEM(v.shape, v.dtype) for v in consts[2:]]
+        + [dma((3,))],
     )
     if not inside:
         data = turned.reshape(4, devices, piece, LANES).transpose(1, 0, 2, 3)

time: 130 us -> 127 us (0.977)
  no operation moved by 1% of the time
where the time goes in v2:
time: 127 us
  waiting for transfers between devices  54 us (43%)
  blocking collectives  49.1 us (39%)
  Pallas kernels  9.58 us (8%)
  starting transfers between devices  7.75 us (6%)
  other arithmetic  5.84 us (5%)
    all_to_all x2, waiting for transfers between devices, exchange(): return lax.all_to_all(value, AXES, split_axis=0, concat_axis=0, tiled=True)  54 us
    all_to_all x2, blocking collectives, exchange(): return lax.all_to_all(value, AXES, split_axis=0, concat_axis=0, tiled=True)  49.1 us
    pallas_call x5, Pallas kernels, call(): pl.pallas_call(kernel, out_shape=outs, in_specs=specs[:len(args)], out_sp...  9.58 us
    all_to_all x2, starting transfers between devices, exchange(): return lax.all_to_all(value, AXES, split_axis=0, concat_axis=0, tiled=True)  7.75 us
    cos x2, other arithmetic, turn(): return (jnp.cos(angle), jnp.sin(angle))  2.9 us
  transfers between devices with their start and end apart: 2, of which 2 were waited for; matrix products, arithmetic and copies ran while one was open for 5% of the time, Pallas kernels for 0%

profile of v2, /device:TPU:0, one launch (start us, length us, event | category | flops | bytes accessed | tf_op | source)
XLA Modules:
  0.0 127.0 jit_solution(881393928938740938)
XLA Ops:
  0.6 1.3 %stack.13 = f32[32,7,8,128]{3,2,1,0:T(8,128)S(1)} custom-call(f32[32,8,128]{2,1,0:T(8,128)} %bitcast.9, f32[32,8,128]{2,1,0:T(8,128)} %bitcast.10, f32[32,8,128]{2,1,0:T(8,128)} %bitcast.11, f32[32,8,128]{2,1,0:T(8,128)} %bitcast.12, f32[32,8,128]{2,1,0:T(8,128)} %bitcast.13, f32[32,8,128]{2,1,0:T(8,128)} %bitcast.14, f32[32,8,128]{2,1,0:T(8,128)} %bitcast.15), custom_call_target="tpu_custom_call" | custom-call | tf_op jit(solution)/shard_map/stack/pallas_call | solution.py:249
  1.9 30.5 %all_to_all.20.x_ref = f32[32,7,8,128]{3,2,1,0:T(8,128)S(1)} all-to-all(f32[32,7,8,128]{3,2,1,0:T(8,128)S(1)} %stack.13), channel_id=1, replica_groups=mesh['grp'=4,'lane'=8] {'grp','lane'}, dimensions={0} | all-to-all | bytes 1835008 | tf_op jit(solution)/shard_map/all_to_all | solution.py:261
  32.5 1.5 %spread.1 = f32[32,7,2,8,128]{4,3,2,1,0:T(8,128)} custom-call(f32[32,7,8,128]{3,2,1,0:T(8,128)S(1)} %all_to_all.20.x_ref), custom_call_target="tpu_custom_call" | custom-call | tf_op jit(solution)/shard_map/spread/pallas_call | solution.py:249
  34.0 3.6 %all-to-all-start.1 = ((f32[32,7,2,8,128]{4,3,2,1,0:T(8,128)}), f32[32,7,2,8,128]{4,3,2,1,0:T(8,128)S(1)}, u32[]{:S(2)}, u32[]{:S(2)}) async-start(f32[32,7,2,8,128]{4,3,2,1,0:T(8,128)} %spread.1), calls=%async_computation.1 | async-start | bytes 3670016 | tf_op jit(solution)/shard_map/all_to_all | solution.py:261
  37.7 1.0 fusion.18
  38.7 0.6 fusion.26
  39.3 0.7 pad_maximum_fusion.4
  40.0 2.3 %fusion.21 = (f32[256,256]{1,0:T(8,128)S(1)}, f32[256,256]{1,0:T(8,128)S(1)}, f32[256,256]{1,0:T(8,128)S(1)}, f32[256,256]{1,0:T(8,128)S(1)}) fusion(s32[256]{0:T(256)S(1)} %iota_multiply_fusion), kind=kLoop, calls=%fused_computation.56 | loop fusion | flops 3276800 | bytes 1049600 | tf_op jit(solution)/shard_map/cos | solution.py:30
  42.3 0.2 fusion
  42.5 0.1 pad_maximum_fusion.a_ref
  42.5 0.9 pad_maximum_fusion.1.ai_far
  43.5 37.3 %all-to-all-done.1.x_ref = f32[32,7,2,8,128]{4,3,2,1,0:T(8,128)S(1)} async-done(((f32[32,7,2,8,128]{4,3,2,1,0:T(8,128)}), f32[32,7,2,8,128]{4,3,2,1,0:T(8,128)S(1)}, u32[]{:S(2)}, u32[]{:S(2)}) %all-to-all-start.1) | async-done | bytes 1835040 | tf_op jit(solution)/shard_map/all_to_all | solution.py:261
  80.7 5.6 %spectrum.1 = f32[32,9,4,128]{3,2,1,0:T(4,128)} custom-call(f32[32,7,2,8,128]{4,3,2,1,0:T(8,128)S(1)} %all-to-all-done.1.x_ref, bf16[512,768]{1,0:T(8,128)(2,1)S(1)} %pad_maximum_fusion.a_ref, f32[2,256,128]{2,1,0:T(8,128)S(1)} %get-tuple-element.20.turn_ref, bf16[2,768,256]{2,1,0:T(8,128)(2,1)} %constant.92.clone.b_far, ...), custom_call_target="tpu_custom_call" | custom-call | tf_op jit(solution)/shard_map/spectrum/pallas_call | solution.py:249
  86.3 4.1 %all-to-all-start.2 = ((f32[32,9,4,128]{3,2,1,0:T(4,128)}), f32[32,9,4,128]{3,2,1,0:T(4,128)S(1)}, u32[]{:S(2)}, u32[]{:S(2)}) async-start(f32[32,9,4,128]{3,2,1,0:T(4,128)} %spectrum.1), calls=%async_computation.2 | async-start | bytes 1179648 | tf_op jit(solution)/shard_map/all_to_all | solution.py:261
  90.5 0.1 multiply_exponential_fusion.last_ref.decay_ref
  90.6 16.7 %all-to-all-done.2.u_ref = f32[32,9,4,128]{3,2,1,0:T(4,128)S(1)} async-done(((f32[32,9,4,128]{3,2,1,0:T(4,128)}), f32[32,9,4,128]{3,2,1,0:T(4,128)S(1)}, u32[]{:S(2)}, u32[]{:S(2)}) %all-to-all-start.2) | async-done | bytes 589856 | tf_op jit(solution)/shard_map/all_to_all | solution.py:261
  107.3 0.3 gather.1
  107.6 18.6 %all_to_all.21.in_ref = f32[32,2,2,8,128]{4,3,2,1,0:T(8,128)S(1)} all-to-all(f32[32,2,2,8,128]{4,3,2,1,0:T(8,128)S(1)} %gather.1), channel_id=1, replica_groups=mesh['grp'=4,'lane'=8] {'grp','lane'}, dimensions={0} | all-to-all | bytes 1048576 | tf_op jit(solution)/shard_map/all_to_all | solution.py:261
  126.2 0.8 deliver.1
  (4 shorter events, 0.0 us)
Async XLA Ops:
  34.0 46.7 %all-to-all-start.1 = ((f32[32,7,2,8,128]{4,3,2,1,0:T(8,128)}), f32[32,7,2,8,128]{4,3,2,1,0:T(8,128)S(1)}, u32[]{:S(2)}, u32[]{:S(2)}) async-start(f32[32,7,2,8,128]{4,3,2,1,0:T(8,128)} %spread.1), calls=%async_computation.1 | async-start | bytes 3670016 | tf_op jit(solution)/shard_map/all_to_all | solution.py:261
  86.3 20.9 %all-to-all-start.2 = ((f32[32,9,4,128]{3,2,1,0:T(4,128)}), f32[32,9,4,128]{3,2,1,0:T(4,128)S(1)}, u32[]{:S(2)}, u32[]{:S(2)}) async-start(f32[32,9,4,128]{3,2,1,0:T(4,128)} %spectrum.1), calls=%async_computation.2 | async-start | bytes 1179648 | tf_op jit(solution)/shard_map/all_to_all | solution.py:261

commit v3 on v2

--- a/solution.py
+++ b/solution.py
@@ -1,3 +1,4 @@
+import functools
 import math
 
 import jax
@@ -11,7 +12,6 @@
 AXES = ("grp", "lane")
 LANES = 128
 FWD_OPS = 7
-CARRY_ROWS = 4
 VMEM = pltpu.MemorySpace.VMEM
 
 
@@ -112,40 +112,17 @@
         copy.wait()
 
 
-def gather_kernel(u_ref, last_ref, decay_ref, out_ref):
+def gather_kernel(u_ref, out_ref):
     devices = u_ref.shape[0]
-    rows = decay_ref.shape[0]
-    packed = len(u_ref.shape) == 4
     for out in range(2):
-
-        def part(slot, which):
-            if not packed:
-                return u_ref[slot, out, which]
-            groups = rows // CARRY_ROWS
-            first = (2 * out + which) * groups
-            return jnp.concatenate([u_ref[slot, first + k] for k in range(groups)], axis=0)
-
-        def last(slot, which):
-            row = 2 * out + which
-            ref = u_ref.at[slot, u_ref.shape[1] - 1] if packed else last_ref.at[slot]
-            return ref[row : row + 1]
-
-        wrap = 0.0
-        for slot in range(devices):
-            angle = 2.0 * math.pi * ((devices - 1) * (4 * slot + 1)) / (4 * devices)
-            wrap = wrap + (math.cos(angle) * last(slot, 1) - math.sin(angle) * last(slot, 0))
-        lane = lax.broadcasted_iota(jnp.int32, wrap.shape, 1)
-        wrap = jnp.sum(jnp.where(lane == LANES - 1, wrap, 0.0), axis=1, keepdims=True)
-        tail = decay_ref[...] * wrap
 
         def load(numer, denom):
             slot = slot_of(numer, denom, devices)
-            return part(slot, 0), part(slot, 1)
+            return u_ref[slot, out, 0], u_ref[slot, out, 1]
 
         for block, pair in enumerate(tree_inverse(devices, 1, 4, load)):
             for k, value in enumerate(pair):
                 index = k * devices + block
-                value = value + math.exp(-0.5 * index) * tail
                 out_ref[index // 2, out, index % 2] = value
 
 
@@ -157,9 +134,14 @@
 
 
 def stack_kernel(*refs):
-    operands, out_ref, sems = refs[:-2], refs[-2], refs[-1]
-    pairs = [(ref, out_ref.at[:, op]) for op, ref in enumerate(operands)]
-    for copy in copy_all(pairs, sems):
+    operands, (out_far, near_ref, in_sems, out_sems) = refs[:-4], refs[-4:]
+    copies = copy_all([(ref, near_ref.at[op]) for op, ref in enumerate(operands)], in_sems)
+    leaving = []
+    for op, copy in enumerate(copies):
+        copy.wait()
+        leaving += [pltpu.make_async_copy(near_ref.at[op], out_far.at[:, op], out_sems.at[op])]
+        leaving[-1].start()
+    for copy in leaving:
         copy.wait()
 
 
@@ -173,12 +155,12 @@
         copy.wait()
 
 
-def spectrum_kernel(
-    x_ref, a_ref, turn_ref, b_far, h_far, ai_far, out_ref,
-    spec_ref, lhs_ref, b_ref, h_ref, ai_ref, sems,
-):
+def spectrum_kernel(x_ref, a_ref, turn_ref, *rest, damp):
+    totals_refs, rest = rest[:-10], rest[-10:]
+    far, (out_ref, spec_ref, lhs_ref), near, sems = rest[:3], rest[3:6], rest[6:9], rest[9]
+    b_ref, h_ref, ai_ref = near
     rows = turn_ref.shape[1]
-    copies = copy_all([(b_far, b_ref), (h_far, h_ref), (ai_far, ai_ref)], sems)
+    copies = copy_all(list(zip(far, near)), sems)
 
     def column_stage(table_ref, re, im):
         both = dot32(table_ref[...], tall_right(split16(jnp.concatenate([re, im], axis=1))))
@@ -195,26 +177,15 @@
         )
         lhs_ref[op] = wide_left(split16(turned))
 
-    for copy in copies:
-        copy.wait()
+    copies[0].wait()
     shape = spec_ref.shape
     left = lhs_ref[...].reshape(shape[0] * shape[1], lhs_ref.shape[2])
     spec_ref[...] = dot32(left, b_ref[0]).reshape(shape)
-
-    def store(out, which, value):
-        if len(out_ref.shape) == 5:
-            out_ref[:, out, which] = value.reshape((out_ref.shape[0],) + out_ref.shape[3:])
-            return
-        devices = out_ref.shape[0]
-        groups = rows // devices // CARRY_ROWS
-        value = value.reshape(devices, groups * CARRY_ROWS, LANES)
-        for k in range(groups):
-            part = value[:, k * CARRY_ROWS : (k + 1) * CARRY_ROWS]
-            out_ref[:, (2 * out + which) * groups + k] = part
-        row = value[devices - 1 :, groups * CARRY_ROWS - 1 :]
-        out_ref[:, 4 * groups, pl.ds(2 * out + which, 1)] = jnp.broadcast_to(
-            row, (devices, 1, LANES)
-        ).reshape(devices, 1, LANES)
+    for copy in copies[1:]:
+        copy.wait()
+
+    totals = sum(ref[...] for ref in totals_refs)
+    totals = damp * jnp.sum(totals, axis=1, keepdims=True)
 
     def member(op):
         return spec_ref[op, :, :LANES], spec_ref[op, :, LANES:]
@@ -230,6 +201,7 @@
 
     for out, pairs in enumerate((((2, 1), (0, 3)), ((4, 1), (0, 5), (6, 3)))):
         re, im = products(pairs)
+        re = re + sum(totals[a : a + 1] * totals[b : b + 1] for a, b in pairs)
         h_re, h_im = h_ref[0], h_ref[1]
         damped = jnp.concatenate([re * h_re - im * h_im, re * h_im + im * h_re], axis=1)
         both = dot32(wide_left(split16(damped)), b_ref[1])
@@ -238,7 +210,8 @@
         re, im = re * turn_re + im * turn_im, im * turn_re - re * turn_im
         re, im = column_stage(ai_ref, re, im)
         for which, value in enumerate((re, im)):
-            store(out, which, value)
+            piece = (out_ref.shape[0],) + out_ref.shape[3:]
+            out_ref[:, out, which] = value.reshape(piece)
 
 
 def call(kernel, name, out_shapes, *args, near, scratch=()):
@@ -304,6 +277,41 @@
     return forward, between, filt, backward
 
 
+def weighted_sums(stacked, rate):
+    local_limbs = stacked.shape[0] * stacked.shape[2] * LANES
+    shape = (stacked.shape[0], 1, stacked.shape[2], LANES)
+    index = (
+        lax.broadcasted_iota(jnp.int32, shape, 0) * shape[2]
+        + lax.broadcasted_iota(jnp.int32, shape, 2)
+    ) * LANES + lax.broadcasted_iota(jnp.int32, shape, 3)
+    left = (local_limbs - 1 - index) + (device_count() - 1 - device_position()) * local_limbs
+    return jnp.sum(stacked * jnp.exp(left.astype(jnp.float32) * -rate), axis=(0, 2))
+
+
+def sum_over_lanes(sums):
+    count = lax.axis_size("lane")
+    step = 1
+    while step < count:
+        sums = sums + lax.ppermute(sums, "lane", [(d, d ^ step) for d in range(count)])
+        step *= 2
+    return sums
+
+
+def group_parts(sums):
+    count = lax.axis_size("grp")
+    step = 1
+    parts = [sums]
+    while step < count:
+        sums = sum(parts[1:], parts[0])
+        span = min(4, count // step)
+        parts = [sums] + [
+            lax.ppermute(sums, "grp", [(d, d ^ (step * k)) for d in range(count)])
+            for k in range(1, span)
+        ]
+        step *= span
+    return parts
+
+
 def local(*operands):
     devices = device_count()
     local_limbs = operands[0].shape[0]
@@ -321,16 +329,20 @@
         "stack",
         [(devices, FWD_OPS, piece, LANES)],
         *far_ops,
-        near=[False] * FWD_OPS + [True],
-        scratch=[dma((FWD_OPS,))],
+        near=[False] * (FWD_OPS + 1),
+        scratch=[
+            pltpu.VMEM((FWD_OPS, devices, piece, LANES), jnp.float32),
+            dma((FWD_OPS,)),
+            dma((FWD_OPS,)),
+        ],
     )
     received = exchange(stacked)
+    sums = sum_over_lanes(weighted_sums(stacked, rate))
+    received, sums = lax.optimization_barrier((received, sums))
     forward, between, filt, backward = tables(local_limbs, devices, scaling / total, rate)
-    consts = (forward, between, lane_tables(), filt, backward)
-    shape = (piece, LANES)
-    index = (device_position() * piece + lax.broadcasted_iota(jnp.int32, shape, 0)) * LANES
-    index = index + lax.broadcasted_iota(jnp.int32, shape, 1)
-    decay = jnp.exp((index + 1).astype(jnp.float32) * -rate)
+    parts = group_parts(sums)
+    near_consts = (forward, between, *parts)
+    far_consts = (lane_tables(), filt, backward)
 
     (spread,) = call(
         spread_kernel,
@@ -346,38 +358,26 @@
     landed = exchange(spread)
     if not inside:
         landed = landed.transpose(1, 2, 0, 3, 4).reshape(1, FWD_OPS, 2, rows, LANES)
-    groups = 4 * piece // CARRY_ROWS
-    packed = (devices, groups + 1, CARRY_ROWS, LANES)
     (turned,) = call(
-        spectrum_kernel,
+        functools.partial(spectrum_kernel, damp=math.exp(-rate)),
         "spectrum",
-        [packed if inside else (1, 2, 2, rows, LANES)],
+        [(devices, 2, 2, piece, LANES) if inside else (1, 2, 2, rows, LANES)],
         landed,
-        *consts,
-        near=[True] * 3 + [False] * 3 + [True],
+        *near_consts,
+        *far_consts,
+        near=[True] * (1 + len(near_consts)) + [False] * 3 + [True],
         scratch=[
             pltpu.VMEM((FWD_OPS, rows, 2 * LANES), jnp.float32),
             pltpu.VMEM((FWD_OPS, rows, 6 * LANES), jnp.bfloat16),
         ]
-        + [pltpu.VMEM(v.shape, v.dtype) for v in consts[2:]]
+        + [pltpu.VMEM(v.shape, v.dtype) for v in far_consts]
         + [dma((3,))],
     )
     if not inside:
-        data = turned.reshape(4, devices, piece, LANES).transpose(1, 0, 2, 3)
-        last = jnp.broadcast_to(turned[0, :, :, -1].reshape(1, 1, 4, LANES), (devices, 1, 4, LANES))
-        turned = jnp.concatenate([data.reshape(devices, groups, CARRY_ROWS, LANES), last], axis=1)
+        turned = turned.reshape(2, 2, devices, piece, LANES).transpose(2, 0, 1, 3, 4)
     gathered = exchange(turned)
-    last = gathered[:, groups] if not inside else decay
-    if not inside:
-        gathered = gathered[:, :groups].reshape(devices, 2, 2, piece, LANES)
     (coeffs,) = call(
-        gather_kernel,
-        "gather",
-        [(devices, 2, 2, piece, LANES)],
-        gathered,
-        last,
-        decay,
-        near=[True] * 4,
+        gather_kernel, "gather", [(devices, 2, 2, piece, LANES)], gathered, near=[True] * 2
     )
     owned = exchange(coeffs)
     results = call(

time: 127 us -> 126 us (level)
  starting transfers between devices: 7.75 us -> 20.6 us
  blocking collectives: 49.1 us -> 37.9 us
  waiting for transfers between devices: 54 us -> 51.1 us
    all_to_all x2, waiting for transfers between devices: 54 us -> 12.7 us  [exchange(): return lax.all_to_all(value, AXES, split_axis=0, concat_axis=0, tiled=True)]
    ppermute x0 -> x6, waiting for transfers between devices: none -> 38.4 us  [the longest x3 33.1 us: group_parts(): lax.ppermute(sums, 'grp', [(d, d ^ step * k) for d in range(count)])]
    all_to_all x2, blocking collectives: 49.1 us -> 37.9 us  [exchange(): return lax.all_to_all(value, AXES, split_axis=0, concat_axis=0, tiled=True)]
    ppermute x0 -> x6, starting transfers between devices: none -> 9.63 us  [the longest x3 5.18 us: sum_over_lanes(): lax.ppermute(sums, 'lane', [(d, d ^ step) for d in range(count)])]
    all_to_all x2, starting transfers between devices: 7.75 us -> 11 us  [exchange(): return lax.all_to_all(value, AXES, split_axis=0, concat_axis=0, tiled=True)]
  transfers between devices with their start and end apart: 2 -> 8, of which waited for: 2 -> 6; matrix products, arithmetic and copies ran while one was open for 5% -> 5% of each run, Pallas kernels for 0% -> 0%
where the time goes in v3:
time: 126 us
  waiting for transfers between devices  51.1 us (41%)
  blocking collectives  37.9 us (30%)
  starting transfers between devices  20.6 us (16%)
  Pallas kernels  9.73 us (8%)
  other arithmetic  6.01 us (5%)
    all_to_all x2, blocking collectives, exchange(): return lax.all_to_all(value, AXES, split_axis=0, concat_axis=0, tiled=True)  37.9 us
    ppermute x3, waiting for transfers between devices, group_parts(): lax.ppermute(sums, 'grp', [(d, d ^ step * k) for d in range(count)])  33.1 us
    all_to_all x2, waiting for transfers between devices, exchange(): return lax.all_to_all(value, AXES, split_axis=0, concat_axis=0, tiled=True)  12.7 us
    all_to_all x2, starting transfers between devices, exchange(): return lax.all_to_all(value, AXES, split_axis=0, concat_axis=0, tiled=True)  11 us
    pallas_call x5, Pallas kernels, call(): pl.pallas_call(kernel, out_shape=outs, in_specs=specs[:len(args)], out_sp...  9.73 us
    ppermute x3, waiting for transfers between devices, sum_over_lanes(): lax.ppermute(sums, 'lane', [(d, d ^ step) for d in range(count)])  5.23 us
    ppermute x3, starting transfers between devices, sum_over_lanes(): lax.ppermute(sums, 'lane', [(d, d ^ step) for d in range(count)])  5.18 us
    ppermute x3, starting transfers between devices, group_parts(): lax.ppermute(sums, 'grp', [(d, d ^ step * k) for d in range(count)])  4.45 us
  transfers between devices with their start and end apart: 8, of which 6 were waited for; matrix products, arithmetic and copies ran while one was open for 5% of the time, Pallas kernels for 0%

profile of v3, /device:TPU:0, one launch (start us, length us, event | category | flops | bytes accessed | tf_op | source)
XLA Modules:
  0.0 126.1 jit_solution(5625927082486755684)
XLA Ops:
  0.6 2.1 %stack.13 = f32[32,7,8,128]{3,2,1,0:T(8,128)} custom-call(f32[32,8,128]{2,1,0:T(8,128)} %bitcast.9, f32[32,8,128]{2,1,0:T(8,128)} %bitcast.10, f32[32,8,128]{2,1,0:T(8,128)} %bitcast.11, f32[32,8,128]{2,1,0:T(8,128)} %bitcast.12, f32[32,8,128]{2,1,0:T(8,128)} %bitcast.13, f32[32,8,128]{2,1,0:T(8,128)} %bitcast.14, f32[32,8,128]{2,1,0:T(8,128)} %bitcast.15), custom_call_target="tpu_custom_call" | custom-call | tf_op jit(solution)/shard_map/stack/pallas_call | solution.py:222
  2.7 0.0 copy-start
  2.7 7.3 %all-to-all-start = ((f32[32,7,8,128]{3,2,1,0:T(8,128)}), f32[32,7,8,128]{3,2,1,0:T(8,128)S(1)}, u32[]{:S(2)}, u32[]{:S(2)}) async-start(f32[32,7,8,128]{3,2,1,0:T(8,128)} %stack.13), calls=%async_computation | async-start | bytes 1835008 | tf_op jit(solution)/shard_map/all_to_all | solution.py:234
  10.1 0.1 multiply_exponential_fusion
  10.2 0.0 copy-done
  10.2 0.1 multiply_reduce_fusion
  10.3 0.3 collective-permute-start
  10.7 0.9 collective-permute-done
  11.6 1.8 %collective-permute-start.1 = (f32[7,128]{1,0:T(8,128)S(1)}, f32[7,128]{1,0:T(8,128)S(1)}, u32[]{:S(2)}, u32[]{:S(2)}) collective-permute-start(f32[7,128]{1,0:T(8,128)S(1)} %add.187), channel_id=1, source_target_pairs={{0,2},{1,3},{2,0},{3,1},{4,6},{5,7},{6,4},{7,5},{8,10},{9,11},{10,... | collective-permute-start | bytes 10760 | tf_op jit(solution)/shard_map/ppermute | solution.py:295
  13.3 2.7 %collective-permute-done.1 = f32[7,128]{1,0:T(8,128)S(1)} collective-permute-done((f32[7,128]{1,0:T(8,128)S(1)}, f32[7,128]{1,0:T(8,128)S(1)}, u32[]{:S(2)}, u32[]{:S(2)}) %collective-permute-start.1) | collective-permute-done | bytes 3616 | tf_op jit(solution)/shard_map/ppermute | solution.py:295
  16.0 3.1 %collective-permute-start.2 = (f32[7,128]{1,0:T(8,128)S(1)}, f32[7,128]{1,0:T(8,128)S(1)}, u32[]{:S(2)}, u32[]{:S(2)}) collective-permute-start(f32[7,128]{1,0:T(8,128)S(1)} %add.188), channel_id=1, source_target_pairs={{0,4},{1,5},{2,6},{3,7},{4,0},{5,1},{6,2},{7,3},{8,12},{9,13},{10,... | collective-permute-start | bytes 10760 | tf_op jit(solution)/shard_map/ppermute | solution.py:295
  19.1 1.6 %collective-permute-done.2 = f32[7,128]{1,0:T(8,128)S(1)} collective-permute-done((f32[7,128]{1,0:T(8,128)S(1)}, f32[7,128]{1,0:T(8,128)S(1)}, u32[]{:S(2)}, u32[]{:S(2)}) %collective-permute-start.2) | collective-permute-done | bytes 3616 | tf_op jit(solution)/shard_map/ppermute | solution.py:295
  20.8 12.7 %all-to-all-done.x_ref = f32[32,7,8,128]{3,2,1,0:T(8,128)S(1)} async-done(((f32[32,7,8,128]{3,2,1,0:T(8,128)}), f32[32,7,8,128]{3,2,1,0:T(8,128)S(1)}, u32[]{:S(2)}, u32[]{:S(2)}) %all-to-all-start) | async-done | bytes 917536 | tf_op jit(solution)/shard_map/all_to_all | solution.py:234
  33.5 1.5 %spread.1 = f32[32,7,2,8,128]{4,3,2,1,0:T(8,128)} custom-call(f32[32,7,8,128]{3,2,1,0:T(8,128)S(1)} %all-to-all-done.x_ref), custom_call_target="tpu_custom_call" | custom-call | tf_op jit(solution)/shard_map/spread/pallas_call | solution.py:222
  35.0 3.6 %all-to-all-start.1 = ((f32[32,7,2,8,128]{4,3,2,1,0:T(8,128)}), f32[32,7,2,8,128]{4,3,2,1,0:T(8,128)S(1)}, u32[]{:S(2)}, u32[]{:S(2)}) async-start(f32[32,7,2,8,128]{4,3,2,1,0:T(8,128)} %spread.1), calls=%async_computation.1 | async-start | bytes 3670016 | tf_op jit(solution)/shard_map/all_to_all | solution.py:234
  38.7 2.3 %fusion.21 = (f32[256,256]{1,0:T(8,128)S(1)}, f32[256,256]{1,0:T(8,128)S(1)}, f32[256,256]{1,0:T(8,128)S(1)}, f32[256,256]{1,0:T(8,128)S(1)}) fusion(s32[256]{0:T(256)S(1)} %iota_multiply_fusion), kind=kLoop, calls=%fused_computation.57 | loop fusion | flops 3276800 | bytes 1049600 | tf_op jit(solution)/shard_map/cos | solution.py:30
  41.0 0.2 fusion
  41.1 0.1 pad_maximum_fusion.a_ref
  41.2 0.9 pad_maximum_fusion.1.rest_6_
  42.1 0.9 fusion.18
  43.1 0.6 fusion.26
  43.7 1.8 %collective-permute-start.3 = (f32[7,128]{1,0:T(8,128)S(1)}, f32[7,128]{1,0:T(8,128)S(1)}, u32[]{:S(2)}, u32[]{:S(2)}) collective-permute-start(f32[7,128]{1,0:T(8,128)S(1)} %add.189.rest_0_), channel_id=1, source_target_pairs={{0,8},{8,0},{16,24},{24,16},{1,9},{9,1},{17,25},{25,17},{2,10},{10... | collective-permute-start | bytes 10760 | tf_op jit(solution)/shard_map/ppermute | solution.py:308
  45.5 2.4 %collective-permute-start.4 = (f32[7,128]{1,0:T(8,128)S(1)}, f32[7,128]{1,0:T(8,128)S(1)}, u32[]{:S(2)}, u32[]{:S(2)}) collective-permute-start(f32[7,128]{1,0:T(8,128)S(1)} %add.189.rest_0_), channel_id=1, source_target_pairs={{0,16},{8,24},{16,0},{24,8},{1,17},{9,25},{17,1},{25,9},{2,18},{10... | collective-permute-start | bytes 10760 | tf_op jit(solution)/shard_map/ppermute | solution.py:308
  48.0 0.2 collective-permute-start.5
  48.2 0.7 pad_maximum_fusion.4
  48.9 20.9 %collective-permute-done.3.rest_1_ = f32[7,128]{1,0:T(8,128)S(1)} collective-permute-done((f32[7,128]{1,0:T(8,128)S(1)}, f32[7,128]{1,0:T(8,128)S(1)}, u32[]{:S(2)}, u32[]{:S(2)}) %collective-permute-start.3) | collective-permute-done | bytes 3616 | tf_op jit(solution)/shard_map/ppermute | solution.py:308
  69.8 12.2 %collective-permute-done.4.rest_2_ = f32[7,128]{1,0:T(8,128)S(1)} collective-permute-done((f32[7,128]{1,0:T(8,128)S(1)}, f32[7,128]{1,0:T(8,128)S(1)}, u32[]{:S(2)}, u32[]{:S(2)}) %collective-permute-start.4) | collective-permute-done | bytes 3616 | tf_op jit(solution)/shard_map/ppermute | solution.py:308
  82.0 0.0 collective-permute-done.5.rest_3_
  82.0 0.0 all-to-all-done.1.x_ref
  82.0 5.1 %spectrum.1 = f32[32,2,2,8,128]{4,3,2,1,0:T(8,128)S(1)} custom-call(f32[32,7,2,8,128]{4,3,2,1,0:T(8,128)S(1)} %all-to-all-done.1.x_ref, bf16[512,768]{1,0:T(8,128)(2,1)S(1)} %pad_maximum_fusion.a_ref, f32[2,256,128]{2,1,0:T(8,128)S(1)} %get-tuple-element.24.turn_ref, f32[7,128]{1,0:T(8,128)S(1)} %add.189.rest_0_, ...), custom_call_target="tpu_custom_call" | custom-call | tf_op jit(solution)/shard_map/spectrum/pallas_call | solution.py:222
  87.1 19.5 %all_to_all.20.u_ref = f32[32,2,2,8,128]{4,3,2,1,0:T(8,128)S(1)} all-to-all(f32[32,2,2,8,128]{4,3,2,1,0:T(8,128)S(1)} %spectrum.1), channel_id=1, replica_groups=mesh['grp'=4,'lane'=8] {'grp','lane'}, dimensions={0} | all-to-all | bytes 1048576 | tf_op jit(solution)/shard_map/all_to_all | solution.py:234
  106.7 0.2 gather.1
  106.9 18.4 %all_to_all.21.in_ref = f32[32,2,2,8,128]{4,3,2,1,0:T(8,128)S(1)} all-to-all(f32[32,2,2,8,128]{4,3,2,1,0:T(8,128)S(1)} %gather.1), channel_id=1, replica_groups=mesh['grp'=4,'lane'=8] {'grp','lane'}, dimensions={0} | all-to-all | bytes 1048576 | tf_op jit(solution)/shard_map/all_to_all | solution.py:234
  125.3 0.8 deliver.1
  (7 shorter events, 0.0 us)
Async XLA Ops:
  2.7 7.5 %copy-start = (f32[32,7,8,128]{3,2,1,0:T(8,128)S(1)}, f32[32,7,8,128]{3,2,1,0:T(8,128)}, u32[]{:S(2)}) copy-start(f32[32,7,8,128]{3,2,1,0:T(8,128)} %stack.13) | copy-start | bytes 2752516
  2.7 30.7 %all-to-all-start = ((f32[32,7,8,128]{3,2,1,0:T(8,128)}), f32[32,7,8,128]{3,2,1,0:T(8,128)S(1)}, u32[]{:S(2)}, u32[]{:S(2)}) async-start(f32[32,7,8,128]{3,2,1,0:T(8,128)} %stack.13), calls=%async_computation | async-start | bytes 1835008 | tf_op jit(solution)/shard_map/all_to_all | solution.py:234
  10.3 1.2 collective-permute-start
  11.6 4.5 %collective-permute-start.1 = (f32[7,128]{1,0:T(8,128)S(1)}, f32[7,128]{1,0:T(8,128)S(1)}, u32[]{:S(2)}, u32[]{:S(2)}) collective-permute-start(f32[7,128]{1,0:T(8,128)S(1)} %add.187), channel_id=1, source_target_pairs={{0,2},{1,3},{2,0},{3,1},{4,6},{5,7},{6,4},{7,5},{8,10},{9,11},{10,... | collective-permute-start | bytes 10760 | tf_op jit(solution)/shard_map/ppermute | solution.py:295
  16.0 4.7 %collective-permute-start.2 = (f32[7,128]{1,0:T(8,128)S(1)}, f32[7,128]{1,0:T(8,128)S(1)}, u32[]{:S(2)}, u32[]{:S(2)}) collective-permute-start(f32[7,128]{1,0:T(8,128)S(1)} %add.188), channel_id=1, source_target_pairs={{0,4},{1,5},{2,6},{3,7},{4,0},{5,1},{6,2},{7,3},{8,12},{9,13},{10,... | collective-permute-start | bytes 10760 | tf_op jit(solution)/shard_map/ppermute | solution.py:295
  35.0 47.0 %all-to-all-start.1 = ((f32[32,7,2,8,128]{4,3,2,1,0:T(8,128)}), f32[32,7,2,8,128]{4,3,2,1,0:T(8,128)S(1)}, u32[]{:S(2)}, u32[]{:S(2)}) async-start(f32[32,7,2,8,128]{4,3,2,1,0:T(8,128)} %spread.1), calls=%async_computation.1 | async-start | bytes 3670016 | tf_op jit(solution)/shard_map/all_to_all | solution.py:234
  43.7 26.1 %collective-permute-start.3 = (f32[7,128]{1,0:T(8,128)S(1)}, f32[7,128]{1,0:T(8,128)S(1)}, u32[]{:S(2)}, u32[]{:S(2)}) collective-permute-start(f32[7,128]{1,0:T(8,128)S(1)} %add.189.rest_0_), channel_id=1, source_target_pairs={{0,8},{8,0},{16,24},{24,16},{1,9},{9,1},{17,25},{25,17},{2,10},{10... | collective-permute-start | bytes 10760 | tf_op jit(solution)/shard_map/ppermute | solution.py:308
  45.5 36.5 %collective-permute-start.4 = (f32[7,128]{1,0:T(8,128)S(1)}, f32[7,128]{1,0:T(8,128)S(1)}, u32[]{:S(2)}, u32[]{:S(2)}) collective-permute-start(f32[7,128]{1,0:T(8,128)S(1)} %add.189.rest_0_), channel_id=1, source_target_pairs={{0,16},{8,24},{16,0},{24,8},{1,17},{9,25},{17,1},{25,9},{2,18},{10... | collective-permute-start | bytes 10760 | tf_op jit(solution)/shard_map/ppermute | solution.py:308
  48.0 34.1 %collective-permute-start.5 = (f32[7,128]{1,0:T(8,128)S(1)}, f32[7,128]{1,0:T(8,128)S(1)}, u32[]{:S(2)}, u32[]{:S(2)}) collective-permute-start(f32[7,128]{1,0:T(8,128)S(1)} %add.189.rest_0_), channel_id=1, source_target_pairs={{0,24},{8,16},{16,8},{24,0},{1,25},{9,17},{17,9},{25,1},{2,26},{10... | collective-permute-start | bytes 10760 | tf_op jit(solution)/shard_map/ppermute | solution.py:308

commit v4 on v3

--- a/solution.py
+++ b/solution.py
@@ -134,14 +134,9 @@
 
 
 def stack_kernel(*refs):
-    operands, (out_far, near_ref, in_sems, out_sems) = refs[:-4], refs[-4:]
-    copies = copy_all([(ref, near_ref.at[op]) for op, ref in enumerate(operands)], in_sems)
-    leaving = []
-    for op, copy in enumerate(copies):
-        copy.wait()
-        leaving += [pltpu.make_async_copy(near_ref.at[op], out_far.at[:, op], out_sems.at[op])]
-        leaving[-1].start()
-    for copy in leaving:
+    operands, out_ref, sems = refs[:-2], refs[-2], refs[-1]
+    pairs = [(ref, out_ref.at[:, op]) for op, ref in enumerate(operands)]
+    for copy in copy_all(pairs, sems):
         copy.wait()
 
 
@@ -277,15 +272,14 @@
     return forward, between, filt, backward
 
 
-def weighted_sums(stacked, rate):
-    local_limbs = stacked.shape[0] * stacked.shape[2] * LANES
-    shape = (stacked.shape[0], 1, stacked.shape[2], LANES)
-    index = (
-        lax.broadcasted_iota(jnp.int32, shape, 0) * shape[2]
-        + lax.broadcasted_iota(jnp.int32, shape, 2)
-    ) * LANES + lax.broadcasted_iota(jnp.int32, shape, 3)
-    left = (local_limbs - 1 - index) + (device_count() - 1 - device_position()) * local_limbs
-    return jnp.sum(stacked * jnp.exp(left.astype(jnp.float32) * -rate), axis=(0, 2))
+def weighted_sums(received, rate):
+    devices, _, piece, _ = received.shape
+    shape = (devices, 1, piece, LANES)
+    index = lax.broadcasted_iota(jnp.int32, shape, 2) + device_position() * piece
+    index = index + lax.broadcasted_iota(jnp.int32, shape, 0) * (devices * piece)
+    index = index * LANES + lax.broadcasted_iota(jnp.int32, shape, 3)
+    left = devices * devices * piece * LANES - 1 - index
+    return jnp.sum(received * jnp.exp(left.astype(jnp.float32) * -rate), axis=(0, 2))
 
 
 def sum_over_lanes(sums):
@@ -329,16 +323,11 @@
         "stack",
         [(devices, FWD_OPS, piece, LANES)],
         *far_ops,
-        near=[False] * (FWD_OPS + 1),
-        scratch=[
-            pltpu.VMEM((FWD_OPS, devices, piece, LANES), jnp.float32),
-            dma((FWD_OPS,)),
-            dma((FWD_OPS,)),
-        ],
+        near=[False] * FWD_OPS + [True],
+        scratch=[dma((FWD_OPS,))],
     )
     received = exchange(stacked)
-    sums = sum_over_lanes(weighted_sums(stacked, rate))
-    received, sums = lax.optimization_barrier((received, sums))
+    sums = sum_over_lanes(weighted_sums(received, rate))
     forward, between, filt, backward = tables(local_limbs, devices, scaling / total, rate)
     parts = group_parts(sums)
     near_consts = (forward, between, *parts)

time: 126 us -> 125 us (level)
  blocking collectives: 37.9 us -> 68.5 us
  waiting for transfers between devices: 51.1 us -> 26.5 us
  starting transfers between devices: 20.6 us -> 14.5 us
    all_to_all x2 -> x3, blocking collectives: 37.9 us -> 68.5 us  [exchange(): return lax.all_to_all(value, AXES, split_axis=0, concat_axis=0, tiled=True)]
    ppermute x3, waiting for transfers between devices: 33.1 us -> 20.2 us  [group_parts(): lax.ppermute(sums, 'grp', [(d, d ^ step * k) for d in range(count)])]
    all_to_all x2 -> x1, waiting for transfers between devices: 12.7 us -> 0.01 us  [exchange(): return lax.all_to_all(value, AXES, split_axis=0, concat_axis=0, tiled=True)]
    all_to_all x2 -> x1, starting transfers between devices: 11 us -> 3.63 us  [exchange(): return lax.all_to_all(value, AXES, split_axis=0, concat_axis=0, tiled=True)]
    ppermute x3, starting transfers between devices: 4.45 us -> 6.42 us  [group_parts(): lax.ppermute(sums, 'grp', [(d, d ^ step * k) for d in range(count)])]
  transfers between devices with their start and end apart: 8 -> 7, of which waited for: 6 -> 5; matrix products, arithmetic and copies ran while one was open for 5% -> 5% of each run, Pallas kernels for 0% -> 0%
where the time goes in v4:
time: 125 us
  blocking collectives  68.5 us (55%)
  waiting for transfers between devices  26.5 us (21%)
  starting transfers between devices  14.5 us (12%)
  Pallas kernels  8.91 us (7%)
  other arithmetic  5.99 us (5%)
    all_to_all x3, blocking collectives, exchange(): return lax.all_to_all(value, AXES, split_axis=0, concat_axis=0, tiled=True)  68.5 us
    ppermute x3, waiting for transfers between devices, group_parts(): lax.ppermute(sums, 'grp', [(d, d ^ step * k) for d in range(count)])  20.2 us
    pallas_call x5, Pallas kernels, call(): pl.pallas_call(kernel, out_shape=outs, in_specs=specs[:len(args)], out_sp...  8.91 us
    ppermute x3, starting transfers between devices, group_parts(): lax.ppermute(sums, 'grp', [(d, d ^ step * k) for d in range(count)])  6.42 us
    ppermute x3, waiting for transfers between devices, sum_over_lanes(): lax.ppermute(sums, 'lane', [(d, d ^ step) for d in range(count)])  6.26 us
    ppermute x3, starting transfers between devices, sum_over_lanes(): lax.ppermute(sums, 'lane', [(d, d ^ step) for d in range(count)])  4.5 us
    all_to_all x1, starting transfers between devices, exchange(): return lax.all_to_all(value, AXES, split_axis=0, concat_axis=0, tiled=True)  3.63 us
    cos x2, other arithmetic, turn(): return (jnp.cos(angle), jnp.sin(angle))  2.9 us
  transfers between devices with their start and end apart: 7, of which 5 were waited for; matrix products, arithmetic and copies ran while one was open for 5% of the time, Pallas kernels for 0%

profile of v4, /device:TPU:0, one launch (start us, length us, event | category | flops | bytes accessed | tf_op | source)
XLA Modules:
  0.0 125.1 jit_solution(8099132898957399746)
XLA Ops:
  0.6 1.3 %stack.13 = f32[32,7,8,128]{3,2,1,0:T(8,128)S(1)} custom-call(f32[32,8,128]{2,1,0:T(8,128)} %bitcast.9, f32[32,8,128]{2,1,0:T(8,128)} %bitcast.10, f32[32,8,128]{2,1,0:T(8,128)} %bitcast.11, f32[32,8,128]{2,1,0:T(8,128)} %bitcast.12, f32[32,8,128]{2,1,0:T(8,128)} %bitcast.13, f32[32,8,128]{2,1,0:T(8,128)} %bitcast.14, f32[32,8,128]{2,1,0:T(8,128)} %bitcast.15), custom_call_target="tpu_custom_call" | custom-call | tf_op jit(solution)/shard_map/stack/pallas_call | solution.py:217
  1.9 30.5 %all_to_all.20.x_ref = f32[32,7,8,128]{3,2,1,0:T(8,128)S(1)} all-to-all(f32[32,7,8,128]{3,2,1,0:T(8,128)S(1)} %stack.13), channel_id=1, replica_groups=mesh['grp'=4,'lane'=8] {'grp','lane'}, dimensions={0} | all-to-all | bytes 1835008 | tf_op jit(solution)/shard_map/all_to_all | solution.py:229
  32.5 1.5 %spread.1 = f32[32,7,2,8,128]{4,3,2,1,0:T(8,128)} custom-call(f32[32,7,8,128]{3,2,1,0:T(8,128)S(1)} %all_to_all.20.x_ref), custom_call_target="tpu_custom_call" | custom-call | tf_op jit(solution)/shard_map/spread/pallas_call | solution.py:217
  34.0 3.6 %all-to-all-start.1 = ((f32[32,7,2,8,128]{4,3,2,1,0:T(8,128)}), f32[32,7,2,8,128]{4,3,2,1,0:T(8,128)S(1)}, u32[]{:S(2)}, u32[]{:S(2)}) async-start(f32[32,7,2,8,128]{4,3,2,1,0:T(8,128)} %spread.1), calls=%async_computation.1 | async-start | bytes 3670016 | tf_op jit(solution)/shard_map/all_to_all | solution.py:229
  37.7 0.1 multiply_exponential_fusion
  37.8 1.0 fusion.18
  38.8 0.6 fusion.26
  39.4 2.3 %fusion.21 = (f32[256,256]{1,0:T(8,128)S(1)}, f32[256,256]{1,0:T(8,128)S(1)}, f32[256,256]{1,0:T(8,128)S(1)}, f32[256,256]{1,0:T(8,128)S(1)}) fusion(s32[256]{0:T(256)S(1)} %iota_multiply_fusion), kind=kLoop, calls=%fused_computation.58 | loop fusion | flops 3276800 | bytes 1049600 | tf_op jit(solution)/shard_map/cos | solution.py:30
  41.7 0.1 multiply_reduce_fusion
  41.8 0.3 collective-permute-start
  42.1 0.2 fusion
  42.3 0.8 collective-permute-done
  43.0 1.8 %collective-permute-start.1 = (f32[7,128]{1,0:T(8,128)S(1)}, f32[7,128]{1,0:T(8,128)S(1)}, u32[]{:S(2)}, u32[]{:S(2)}) collective-permute-start(f32[7,128]{1,0:T(8,128)S(1)} %add.190), channel_id=1, source_target_pairs={{0,2},{1,3},{2,0},{3,1},{4,6},{5,7},{6,4},{7,5},{8,10},{9,11},{10,... | collective-permute-start | bytes 10760 | tf_op jit(solution)/shard_map/ppermute | solution.py:289
  44.8 0.1 pad_maximum_fusion.a_ref
  44.9 4.7 %collective-permute-done.1 = f32[7,128]{1,0:T(8,128)S(1)} collective-permute-done((f32[7,128]{1,0:T(8,128)S(1)}, f32[7,128]{1,0:T(8,128)S(1)}, u32[]{:S(2)}, u32[]{:S(2)}) %collective-permute-start.1) | collective-permute-done | bytes 3616 | tf_op jit(solution)/shard_map/ppermute | solution.py:289
  49.6 2.4 %collective-permute-start.2 = (f32[7,128]{1,0:T(8,128)S(1)}, f32[7,128]{1,0:T(8,128)S(1)}, u32[]{:S(2)}, u32[]{:S(2)}) collective-permute-start(f32[7,128]{1,0:T(8,128)S(1)} %add.191), channel_id=1, source_target_pairs={{0,4},{1,5},{2,6},{3,7},{4,0},{5,1},{6,2},{7,3},{8,12},{9,13},{10,... | collective-permute-start | bytes 10760 | tf_op jit(solution)/shard_map/ppermute | solution.py:289
  52.0 0.9 pad_maximum_fusion.1.rest_6_
  53.0 0.8 collective-permute-done.2
  53.7 5.9 %collective-permute-start.5 = (f32[7,128]{1,0:T(8,128)S(1)}, f32[7,128]{1,0:T(8,128)S(1)}, u32[]{:S(2)}, u32[]{:S(2)}) collective-permute-start(f32[7,128]{1,0:T(8,128)S(1)} %add.192.rest_0_), channel_id=1, source_target_pairs={{0,24},{8,16},{16,8},{24,0},{1,25},{9,17},{17,9},{25,1},{2,26},{10... | collective-permute-start | bytes 10760 | tf_op jit(solution)/shard_map/ppermute | solution.py:302
  59.6 0.0 collective-permute-start.4
  59.6 0.6 collective-permute-start.3
  60.2 0.7 pad_maximum_fusion.4
  60.9 11.1 %collective-permute-done.5.rest_3_ = f32[7,128]{1,0:T(8,128)S(1)} collective-permute-done((f32[7,128]{1,0:T(8,128)S(1)}, f32[7,128]{1,0:T(8,128)S(1)}, u32[]{:S(2)}, u32[]{:S(2)}) %collective-permute-start.5) | collective-permute-done | bytes 3616 | tf_op jit(solution)/shard_map/ppermute | solution.py:302
  72.0 9.0 %collective-permute-done.4.rest_2_ = f32[7,128]{1,0:T(8,128)S(1)} collective-permute-done((f32[7,128]{1,0:T(8,128)S(1)}, f32[7,128]{1,0:T(8,128)S(1)}, u32[]{:S(2)}, u32[]{:S(2)}) %collective-permute-start.4) | collective-permute-done | bytes 3616 | tf_op jit(solution)/shard_map/ppermute | solution.py:302
  81.1 0.0 collective-permute-done.3.rest_1_
  81.1 0.0 all-to-all-done.1.x_ref
  81.1 5.0 %spectrum.1 = f32[32,2,2,8,128]{4,3,2,1,0:T(8,128)S(1)} custom-call(f32[32,7,2,8,128]{4,3,2,1,0:T(8,128)S(1)} %all-to-all-done.1.x_ref, bf16[512,768]{1,0:T(8,128)(2,1)S(1)} %pad_maximum_fusion.a_ref, f32[2,256,128]{2,1,0:T(8,128)S(1)} %get-tuple-element.20.turn_ref, f32[7,128]{1,0:T(8,128)S(1)} %add.192.rest_0_, ...), custom_call_target="tpu_custom_call" | custom-call | tf_op jit(solution)/shard_map/spectrum/pallas_call | solution.py:217
  86.1 19.5 %all_to_all.21.u_ref = f32[32,2,2,8,128]{4,3,2,1,0:T(8,128)S(1)} all-to-all(f32[32,2,2,8,128]{4,3,2,1,0:T(8,128)S(1)} %spectrum.1), channel_id=1, replica_groups=mesh['grp'=4,'lane'=8] {'grp','lane'}, dimensions={0} | all-to-all | bytes 1048576 | tf_op jit(solution)/shard_map/all_to_all | solution.py:229
  105.7 0.2 gather.1
  105.9 18.4 %all_to_all.22.in_ref = f32[32,2,2,8,128]{4,3,2,1,0:T(8,128)S(1)} all-to-all(f32[32,2,2,8,128]{4,3,2,1,0:T(8,128)S(1)} %gather.1), channel_id=1, replica_groups=mesh['grp'=4,'lane'=8] {'grp','lane'}, dimensions={0} | all-to-all | bytes 1048576 | tf_op jit(solution)/shard_map/all_to_all | solution.py:229
  124.3 0.8 deliver.1
  (8 shorter events, 0.0 us)
Async XLA Ops:
  34.0 47.1 %all-to-all-start.1 = ((f32[32,7,2,8,128]{4,3,2,1,0:T(8,128)}), f32[32,7,2,8,128]{4,3,2,1,0:T(8,128)S(1)}, u32[]{:S(2)}, u32[]{:S(2)}) async-start(f32[32,7,2,8,128]{4,3,2,1,0:T(8,128)} %spread.1), calls=%async_computation.1 | async-start | bytes 3670016 | tf_op jit(solution)/shard_map/all_to_all | solution.py:229
  41.8 1.2 collective-permute-start
  43.0 6.6 %collective-permute-start.1 = (f32[7,128]{1,0:T(8,128)S(1)}, f32[7,128]{1,0:T(8,128)S(1)}, u32[]{:S(2)}, u32[]{:S(2)}) collective-permute-start(f32[7,128]{1,0:T(8,128)S(1)} %add.190), channel_id=1, source_target_pairs={{0,2},{1,3},{2,0},{3,1},{4,6},{5,7},{6,4},{7,5},{8,10},{9,11},{10,... | collective-permute-start | bytes 10760 | tf_op jit(solution)/shard_map/ppermute | solution.py:289
  49.6 4.1 %collective-permute-start.2 = (f32[7,128]{1,0:T(8,128)S(1)}, f32[7,128]{1,0:T(8,128)S(1)}, u32[]{:S(2)}, u32[]{:S(2)}) collective-permute-start(f32[7,128]{1,0:T(8,128)S(1)} %add.191), channel_id=1, source_target_pairs={{0,4},{1,5},{2,6},{3,7},{4,0},{5,1},{6,2},{7,3},{8,12},{9,13},{10,... | collective-permute-start | bytes 10760 | tf_op jit(solution)/shard_map/ppermute | solution.py:289
  53.7 18.3 %collective-permute-start.5 = (f32[7,128]{1,0:T(8,128)S(1)}, f32[7,128]{1,0:T(8,128)S(1)}, u32[]{:S(2)}, u32[]{:S(2)}) collective-permute-start(f32[7,128]{1,0:T(8,128)S(1)} %add.192.rest_0_), channel_id=1, source_target_pairs={{0,24},{8,16},{16,8},{24,0},{1,25},{9,17},{17,9},{25,1},{2,26},{10... | collective-permute-start | bytes 10760 | tf_op jit(solution)/shard_map/ppermute | solution.py:302
  59.6 21.5 %collective-permute-start.4 = (f32[7,128]{1,0:T(8,128)S(1)}, f32[7,128]{1,0:T(8,128)S(1)}, u32[]{:S(2)}, u32[]{:S(2)}) collective-permute-start(f32[7,128]{1,0:T(8,128)S(1)} %add.192.rest_0_), channel_id=1, source_target_pairs={{0,16},{8,24},{16,0},{24,8},{1,17},{9,25},{17,1},{25,9},{2,18},{10... | collective-permute-start | bytes 10760 | tf_op jit(solution)/shard_map/ppermute | solution.py:302
  59.6 21.5 %collective-permute-start.3 = (f32[7,128]{1,0:T(8,128)S(1)}, f32[7,128]{1,0:T(8,128)S(1)}, u32[]{:S(2)}, u32[]{:S(2)}) collective-permute-start(f32[7,128]{1,0:T(8,128)S(1)} %add.192.rest_0_), channel_id=1, source_target_pairs={{0,8},{8,0},{16,24},{24,16},{1,9},{9,1},{17,25},{25,17},{2,10},{10... | collective-permute-start | bytes 10760 | tf_op jit(solution)/shard_map/ppermute | solution.py:302

commit v5 on v4

--- a/solution.py
+++ b/solution.py
@@ -150,21 +150,62 @@
         copy.wait()
 
 
-def spectrum_kernel(x_ref, a_ref, turn_ref, *rest, damp):
-    totals_refs, rest = rest[:-10], rest[-10:]
-    far, (out_ref, spec_ref, lhs_ref), near, sems = rest[:3], rest[3:6], rest[6:9], rest[9]
-    b_ref, h_ref, ai_ref = near
+def spectrum_kernel(x_ref, a_ref, ai_ref, turn_ref, h_ref, roots_ref, *rest, damp):
+    totals_refs, (b_far, out_ref, spec_ref, lhs_ref, b_ref, sems) = rest[:-6], rest[-6:]
     rows = turn_ref.shape[1]
-    copies = copy_all(list(zip(far, near)), sems)
-
-    def column_stage(table_ref, re, im):
-        both = dot32(table_ref[...], tall_right(split16(jnp.concatenate([re, im], axis=1))))
-        top, bottom = both[:rows], both[rows:]
+    copies = copy_all([(b_far, b_ref)], sems)
+
+    quarter = rows // 4
+    rho = (roots_ref[0:1], roots_ref[1:2])
+    sigma = (roots_ref[2:3], roots_ref[3:4])
+
+    def times(a, b):
+        return a[0] * b[0] - a[1] * b[1], a[0] * b[1] + a[1] * b[0]
+
+    def times_conj(a, b):
+        return a[0] * b[0] + a[1] * b[1], a[1] * b[0] - a[0] * b[1]
+
+    def add(a, b):
+        return a[0] + b[0], a[1] + b[1]
+
+    def sub(a, b):
+        return a[0] - b[0], a[1] - b[1]
+
+    def section(table, value):
+        high, low = split16(jnp.concatenate(value, axis=1))
+        both = dot32(table, jnp.concatenate([high, low, high, low], axis=0))
+        top, bottom = both[:quarter], both[quarter:]
         return top[:, :LANES] - bottom[:, LANES:], top[:, LANES:] + bottom[:, :LANES]
 
+    def join(values):
+        return tuple(jnp.concatenate([v[k] for v in values], axis=0) for k in range(2))
+
+    def cut(re, im):
+        parts = [slice(m * quarter, (m + 1) * quarter) for m in range(4)]
+        return [(re[part], im[part]) for part in parts]
+
+    def column_forward(re, im):
+        x = cut(re, im)
+        turned = [times(x[2], rho), times(x[3], rho)]
+        plus = [add(x[0], turned[0]), add(x[1], turned[1])]
+        minus = [sub(x[0], turned[0]), sub(x[1], turned[1])]
+        even, odd = times(plus[1], sigma), times(minus[1], sigma)
+        odd = (-odd[1], odd[0])
+        nodes = [add(plus[0], even), add(minus[0], odd), sub(plus[0], even), sub(minus[0], odd)]
+        return join([section(a_ref[j], nodes[j]) for j in range(4)])
+
+    def column_inverse(re, im):
+        nodes = [section(ai_ref[j], value) for j, value in enumerate(cut(re, im))]
+        odd = sub(nodes[1], nodes[3])
+        plus = [add(nodes[0], nodes[2]), times_conj(sub(nodes[0], nodes[2]), sigma)]
+        minus = [add(nodes[1], nodes[3]), times_conj((odd[1], -odd[0]), sigma)]
+        low = [add(plus[m], minus[m]) for m in range(2)]
+        high = [times_conj(sub(plus[m], minus[m]), rho) for m in range(2)]
+        return join(low + high)
+
     for op in range(FWD_OPS):
-        re, im = column_stage(
-            a_ref, x_ref[:, op, 0].reshape(rows, LANES), x_ref[:, op, 1].reshape(rows, LANES)
+        re, im = column_forward(
+            x_ref[:, op, 0].reshape(rows, LANES), x_ref[:, op, 1].reshape(rows, LANES)
         )
         turn_re, turn_im = turn_ref[0], turn_ref[1]
         turned = jnp.concatenate(
@@ -176,8 +217,6 @@
     shape = spec_ref.shape
     left = lhs_ref[...].reshape(shape[0] * shape[1], lhs_ref.shape[2])
     spec_ref[...] = dot32(left, b_ref[0]).reshape(shape)
-    for copy in copies[1:]:
-        copy.wait()
 
     totals = sum(ref[...] for ref in totals_refs)
     totals = damp * jnp.sum(totals, axis=1, keepdims=True)
@@ -203,7 +242,7 @@
         re, im = both[:, :LANES], both[:, LANES:]
         turn_re, turn_im = turn_ref[0], turn_ref[1]
         re, im = re * turn_re + im * turn_im, im * turn_re - re * turn_im
-        re, im = column_stage(ai_ref, re, im)
+        re, im = column_inverse(re, im)
         for which, value in enumerate((re, im)):
             piece = (out_ref.shape[0],) + out_ref.shape[3:]
             out_ref[:, out, which] = value.reshape(piece)
@@ -251,15 +290,24 @@
     def grid(shape):
         return (lax.broadcasted_iota(jnp.int32, shape, 0), lax.broadcasted_iota(jnp.int32, shape, 1))
 
-    q1, t1 = grid((rows, rows))
-    step = period // rows
-    cos, sin = turn(((t1 * q1) % rows) * step + LANES * t1 * freq, period)
-    forward = wide_left(split_table(jnp.concatenate([cos, sin], axis=0)))
-    t1, q1 = grid((rows, rows))
-    cos, sin = turn(((t1 * q1) % rows) * step + LANES * t1 * freq, period)
-    backward = wide_left(split_table(jnp.concatenate([cos, -sin], axis=0)))
-    q1, t2 = grid((rows, LANES))
+    quarter = rows // 4
+
+    def section(conjugate):
+        shape = (4, quarter, quarter)
+        node = lax.broadcasted_iota(jnp.int32, shape, 0)
+        k = lax.broadcasted_iota(jnp.int32, shape, 2 if conjugate else 1)
+        t1 = lax.broadcasted_iota(jnp.int32, shape, 1 if conjugate else 2)
+        cos, sin = turn(t1 * (freq + 4 * devices * (4 * k + node)) * LANES, period)
+        table = jnp.concatenate([cos, -sin if conjugate else sin], axis=1)
+        high, low = split_table(table)
+        return jnp.concatenate([high, high, low, low], axis=2)
+
+    forward, backward = section(False), section(True)
+    row, t2 = grid((rows, LANES))
+    q1 = 4 * (row % quarter) + row // quarter
     between = jnp.stack(turn(t2 * (q1 * (period // local_limbs) + freq), period))
+    spread_freq = freq + lax.broadcasted_iota(jnp.int32, (LANES,), 0) * 0
+    roots = jnp.stack(turn(spread_freq, 8 * devices) + turn(spread_freq, 16 * devices))
     numer = freq + 4 * devices * (q1 + rows * t2)
     numer = jnp.where(2 * numer > period, numer - period, numer)
     angle = numer.astype(jnp.float32) * (2.0 * math.pi / period)
@@ -269,7 +317,7 @@
     den_im = -damp * jnp.sin(angle)
     norm = scaling / (den_re * den_re + den_im * den_im)
     filt = jnp.stack([den_re * norm, -den_im * norm])
-    return forward, between, filt, backward
+    return forward, backward, between, filt, roots
 
 
 def weighted_sums(received, rate):
@@ -328,10 +376,10 @@
     )
     received = exchange(stacked)
     sums = sum_over_lanes(weighted_sums(received, rate))
-    forward, between, filt, backward = tables(local_limbs, devices, scaling / total, rate)
+    near_tables = tables(local_limbs, devices, scaling / total, rate)
     parts = group_parts(sums)
-    near_consts = (forward, between, *parts)
-    far_consts = (lane_tables(), filt, backward)
+    near_consts = (*near_tables, *parts)
+    lane_table = lane_tables()
 
     (spread,) = call(
         spread_kernel,
@@ -353,14 +401,14 @@
         [(devices, 2, 2, piece, LANES) if inside else (1, 2, 2, rows, LANES)],
         landed,
         *near_consts,
-        *far_consts,
-        near=[True] * (1 + len(near_consts)) + [False] * 3 + [True],
+        lane_table,
+        near=[True] * (1 + len(near_consts)) + [False, True],
         scratch=[
             pltpu.VMEM((FWD_OPS, rows, 2 * LANES), jnp.float32),
             pltpu.VMEM((FWD_OPS, rows, 6 * LANES), jnp.bfloat16),
-        ]
-        + [pltpu.VMEM(v.shape, v.dtype) for v in far_consts]
-        + [dma((3,))],
+            pltpu.VMEM(lane_table.shape, lane_table.dtype),
+            dma((1,)),
+        ],
     )
     if not inside:
         turned = turned.reshape(2, 2, devices, piece, LANES).transpose(2, 0, 1, 3, 4)

time: 125 us -> 124 us (level)
  other arithmetic: 5.99 us -> 3.56 us
  waiting for transfers between devices: 26.5 us -> 28.5 us
  Pallas kernels: 8.91 us -> 7.12 us
    pallas_call x5, Pallas kernels: 8.91 us -> 7.12 us  [call(): pl.pallas_call(kernel, out_shape=outs, in_specs=specs[:len(args)], out_sp...]
    cos x2 -> x1, other arithmetic: 2.9 us -> 1.11 us  [turn(): return (jnp.cos(angle), jnp.sin(angle))]
    ppermute x3, waiting for transfers between devices: 6.26 us -> 7.68 us  [sum_over_lanes(): lax.ppermute(sums, 'lane', [(d, d ^ step) for d in range(count)])]
  transfers between devices with their start and end apart: 7 -> 7, of which waited for: 5 -> 5; matrix products, arithmetic and copies ran while one was open for 5% -> 3% of each run, Pallas kernels for 0% -> 0%
where the time goes in v5:
time: 124 us; the launch traced here: 123 us
  blocking collectives  68.5 us (55%)
  waiting for transfers between devices  28.5 us (23%)
  starting transfers between devices  14.5 us (12%)
  Pallas kernels  7.12 us (6%)
  other arithmetic  3.56 us (3%)
    all_to_all x3, blocking collectives, exchange(): return lax.all_to_all(value, AXES, split_axis=0, concat_axis=0, tiled=True)  68.5 us
    ppermute x3, waiting for transfers between devices, group_parts(): lax.ppermute(sums, 'grp', [(d, d ^ step * k) for d in range(count)])  20.8 us
    ppermute x3, waiting for transfers between devices, sum_over_lanes(): lax.ppermute(sums, 'lane', [(d, d ^ step) for d in range(count)])  7.68 us
    pallas_call x5, Pallas kernels, call(): pl.pallas_call(kernel, out_shape=outs, in_specs=specs[:len(args)], out_sp...  7.12 us
    ppermute x3, starting transfers between devices, group_parts(): lax.ppermute(sums, 'grp', [(d, d ^ step * k) for d in range(count)])  6.42 us
    ppermute x3, starting transfers between devices, sum_over_lanes(): lax.ppermute(sums, 'lane', [(d, d ^ step) for d in range(count)])  4.48 us
    all_to_all x1, starting transfers between devices, exchange(): return lax.all_to_all(value, AXES, split_axis=0, concat_axis=0, tiled=True)  3.63 us
  transfers between devices with their start and end apart: 7, of which 5 were waited for; matrix products, arithmetic and copies ran while one was open for 3% of the time, Pallas kernels for 0%

profile of v5, /device:TPU:0, one launch (start us, length us, event | category | flops | bytes accessed | tf_op | source)
XLA Modules:
  0.0 123.3 jit_solution(6493647633612824990)
XLA Ops:
  0.6 1.3 %stack.10 = f32[32,7,8,128]{3,2,1,0:T(8,128)S(1)} custom-call(f32[32,8,128]{2,1,0:T(8,128)} %bitcast.13, f32[32,8,128]{2,1,0:T(8,128)} %bitcast.14, f32[32,8,128]{2,1,0:T(8,128)} %bitcast.15, f32[32,8,128]{2,1,0:T(8,128)} %bitcast.16, f32[32,8,128]{2,1,0:T(8,128)} %bitcast.17, f32[32,8,128]{2,1,0:T(8,128)} %bitcast.18, f32[32,8,128]{2,1,0:T(8,128)} %bitcast.19), custom_call_target="tpu_custom_call" | custom-call | tf_op jit(solution)/shard_map/stack/pallas_call | solution.py:256
  1.9 30.5 %all_to_all.20.x_ref = f32[32,7,8,128]{3,2,1,0:T(8,128)S(1)} all-to-all(f32[32,7,8,128]{3,2,1,0:T(8,128)S(1)} %stack.10), channel_id=1, replica_groups=mesh['grp'=4,'lane'=8] {'grp','lane'}, dimensions={0} | all-to-all | bytes 1835008 | tf_op jit(solution)/shard_map/all_to_all | solution.py:268
  32.5 1.6 %spread.1 = f32[32,7,2,8,128]{4,3,2,1,0:T(8,128)} custom-call(f32[32,7,8,128]{3,2,1,0:T(8,128)S(1)} %all_to_all.20.x_ref), custom_call_target="tpu_custom_call" | custom-call | tf_op jit(solution)/shard_map/spread/pallas_call | solution.py:256
  34.0 3.6 %all-to-all-start.1 = ((f32[32,7,2,8,128]{4,3,2,1,0:T(8,128)}), f32[32,7,2,8,128]{4,3,2,1,0:T(8,128)S(1)}, u32[]{:S(2)}, u32[]{:S(2)}) async-start(f32[32,7,2,8,128]{4,3,2,1,0:T(8,128)} %spread.1), calls=%async_computation.1 | async-start | bytes 3670016 | tf_op jit(solution)/shard_map/all_to_all | solution.py:268
  37.8 1.1 fusion.14
  38.9 0.1 reduce-precision_convert_fusion
  39.0 0.1 multiply_exponential_fusion
  39.1 1.6 %fusion.13 = (f32[1,256,128]{2,1,0:T(8,128)S(1)}, f32[1,256,128]{2,1,0:T(8,128)S(1)}, f32[1,256,128]{2,1,0:T(8,128)S(1)}, f32[1,256,128]{2,1,0:T(8,128)S(1)}) fusion(s32[128]{0:T(128)S(1)} %iota_multiply_fusion.1, s32[]{:T(128)S(6)} %add.239, s32[256]{0:T(256)S(1)} %iota_shift-right-logical_fusion, s32[256]{0:T(256)S(1)} %broadcast_add_fusion, ...), kind=kLoop, calls=%fused_computation.41 | loop fusion | flops 1474560 | bytes 529412 | tf_op jit(solution)/shard_map/mul | solution.py:319
  40.7 0.1 multiply_reduce_fusion
  40.8 0.3 collective-permute-start
  41.2 0.9 collective-permute-done
  42.1 1.8 %collective-permute-start.1 = (f32[7,128]{1,0:T(8,128)S(1)}, f32[7,128]{1,0:T(8,128)S(1)}, u32[]{:S(2)}, u32[]{:S(2)}) collective-permute-start(f32[7,128]{1,0:T(8,128)S(1)} %add.263), channel_id=1, source_target_pairs={{0,2},{1,3},{2,0},{3,1},{4,6},{5,7},{6,4},{7,5},{8,10},{9,11},{10,... | collective-permute-start | bytes 10760 | tf_op jit(solution)/shard_map/ppermute | solution.py:337
  43.8 0.2 pad_maximum_fusion.1.a_ref
  44.0 5.6 %collective-permute-done.1 = f32[7,128]{1,0:T(8,128)S(1)} collective-permute-done((f32[7,128]{1,0:T(8,128)S(1)}, f32[7,128]{1,0:T(8,128)S(1)}, u32[]{:S(2)}, u32[]{:S(2)}) %collective-permute-start.1) | collective-permute-done | bytes 3616 | tf_op jit(solution)/shard_map/ppermute | solution.py:337
  49.6 2.4 %collective-permute-start.2 = (f32[7,128]{1,0:T(8,128)S(1)}, f32[7,128]{1,0:T(8,128)S(1)}, u32[]{:S(2)}, u32[]{:S(2)}) collective-permute-start(f32[7,128]{1,0:T(8,128)S(1)} %add.264), channel_id=1, source_target_pairs={{0,4},{1,5},{2,6},{3,7},{4,0},{5,1},{6,2},{7,3},{8,12},{9,13},{10,... | collective-permute-start | bytes 10760 | tf_op jit(solution)/shard_map/ppermute | solution.py:337
  52.0 0.2 pad_maximum_fusion.3.ai_ref
  52.6 1.2 collective-permute-done.2
  53.8 0.6 collective-permute-start.3
  54.3 5.9 %collective-permute-start.4 = (f32[7,128]{1,0:T(8,128)S(1)}, f32[7,128]{1,0:T(8,128)S(1)}, u32[]{:S(2)}, u32[]{:S(2)}) collective-permute-start(f32[7,128]{1,0:T(8,128)S(1)} %add.265.rest_0_), channel_id=1, source_target_pairs={{0,16},{8,24},{16,0},{24,8},{1,17},{9,25},{17,1},{25,9},{2,18},{10... | collective-permute-start | bytes 10760 | tf_op jit(solution)/shard_map/ppermute | solution.py:350
  60.2 0.0 collective-permute-start.5
  60.2 0.1 maximum_maximum_fusion
  60.3 8.6 %collective-permute-done.3.rest_1_ = f32[7,128]{1,0:T(8,128)S(1)} collective-permute-done((f32[7,128]{1,0:T(8,128)S(1)}, f32[7,128]{1,0:T(8,128)S(1)}, u32[]{:S(2)}, u32[]{:S(2)}) %collective-permute-start.3) | collective-permute-done | bytes 3616 | tf_op jit(solution)/shard_map/ppermute | solution.py:350
  68.8 12.2 %collective-permute-done.4.rest_2_ = f32[7,128]{1,0:T(8,128)S(1)} collective-permute-done((f32[7,128]{1,0:T(8,128)S(1)}, f32[7,128]{1,0:T(8,128)S(1)}, u32[]{:S(2)}, u32[]{:S(2)}) %collective-permute-start.4) | collective-permute-done | bytes 3616 | tf_op jit(solution)/shard_map/ppermute | solution.py:350
  81.1 0.0 collective-permute-done.5.rest_3_
  81.1 0.0 all-to-all-done.1.x_ref
  81.1 0.1 broadcast.940.roots_ref
  81.1 3.2 %spectrum.1 = f32[32,2,2,8,128]{4,3,2,1,0:T(8,128)S(1)} custom-call(f32[32,7,2,8,128]{4,3,2,1,0:T(8,128)S(1)} %all-to-all-done.1.x_ref, bf16[4,128,256]{2,1,0:T(8,128)(2,1)S(1)} %pad_maximum_fusion.1.a_ref, bf16[4,128,256]{2,1,0:T(8,128)(2,1)S(1)} %pad_maximum_fusion.3.ai_ref, f32[2,256,128]{2,1,0:T(8,128)S(1)} %get-tuple-element.20.turn_ref, ...), custom_call_target="tpu_custom_call" | custom-call | tf_op jit(solution)/shard_map/spectrum/pallas_call | solution.py:256
  84.4 19.5 %all_to_all.21.u_ref = f32[32,2,2,8,128]{4,3,2,1,0:T(8,128)S(1)} all-to-all(f32[32,2,2,8,128]{4,3,2,1,0:T(8,128)S(1)} %spectrum.1), channel_id=1, replica_groups=mesh['grp'=4,'lane'=8] {'grp','lane'}, dimensions={0} | all-to-all | bytes 1048576 | tf_op jit(solution)/shard_map/all_to_all | solution.py:268
  103.9 0.2 gather.1
  104.1 18.4 %all_to_all.22.in_ref = f32[32,2,2,8,128]{4,3,2,1,0:T(8,128)S(1)} all-to-all(f32[32,2,2,8,128]{4,3,2,1,0:T(8,128)S(1)} %gather.1), channel_id=1, replica_groups=mesh['grp'=4,'lane'=8] {'grp','lane'}, dimensions={0} | all-to-all | bytes 1048576 | tf_op jit(solution)/shard_map/all_to_all | solution.py:268
  122.5 0.8 deliver.1
  (14 shorter events, 0.1 us)
Async XLA Ops:
  34.0 47.0 %all-to-all-start.1 = ((f32[32,7,2,8,128]{4,3,2,1,0:T(8,128)}), f32[32,7,2,8,128]{4,3,2,1,0:T(8,128)S(1)}, u32[]{:S(2)}, u32[]{:S(2)}) async-start(f32[32,7,2,8,128]{4,3,2,1,0:T(8,128)} %spread.1), calls=%async_computation.1 | async-start | bytes 3670016 | tf_op jit(solution)/shard_map/all_to_all | solution.py:268
  40.8 1.2 collective-permute-start
  42.1 7.6 %collective-permute-start.1 = (f32[7,128]{1,0:T(8,128)S(1)}, f32[7,128]{1,0:T(8,128)S(1)}, u32[]{:S(2)}, u32[]{:S(2)}) collective-permute-start(f32[7,128]{1,0:T(8,128)S(1)} %add.263), channel_id=1, source_target_pairs={{0,2},{1,3},{2,0},{3,1},{4,6},{5,7},{6,4},{7,5},{8,10},{9,11},{10,... | collective-permute-start | bytes 10760 | tf_op jit(solution)/shard_map/ppermute | solution.py:337
  49.6 4.1 %collective-permute-start.2 = (f32[7,128]{1,0:T(8,128)S(1)}, f32[7,128]{1,0:T(8,128)S(1)}, u32[]{:S(2)}, u32[]{:S(2)}) collective-permute-start(f32[7,128]{1,0:T(8,128)S(1)} %add.264), channel_id=1, source_target_pairs={{0,4},{1,5},{2,6},{3,7},{4,0},{5,1},{6,2},{7,3},{8,12},{9,13},{10,... | collective-permute-start | bytes 10760 | tf_op jit(solution)/shard_map/ppermute | solution.py:337
  53.8 15.1 %collective-permute-start.3 = (f32[7,128]{1,0:T(8,128)S(1)}, f32[7,128]{1,0:T(8,128)S(1)}, u32[]{:S(2)}, u32[]{:S(2)}) collective-permute-start(f32[7,128]{1,0:T(8,128)S(1)} %add.265.rest_0_), channel_id=1, source_target_pairs={{0,8},{8,0},{16,24},{24,16},{1,9},{9,1},{17,25},{25,17},{2,10},{10... | collective-permute-start | bytes 10760 | tf_op jit(solution)/shard_map/ppermute | solution.py:350
  54.3 26.7 %collective-permute-start.4 = (f32[7,128]{1,0:T(8,128)S(1)}, f32[7,128]{1,0:T(8,128)S(1)}, u32[]{:S(2)}, u32[]{:S(2)}) collective-permute-start(f32[7,128]{1,0:T(8,128)S(1)} %add.265.rest_0_), channel_id=1, source_target_pairs={{0,16},{8,24},{16,0},{24,8},{1,17},{9,25},{17,1},{25,9},{2,18},{10... | collective-permute-start | bytes 10760 | tf_op jit(solution)/shard_map/ppermute | solution.py:350
  60.2 20.9 %collective-permute-start.5 = (f32[7,128]{1,0:T(8,128)S(1)}, f32[7,128]{1,0:T(8,128)S(1)}, u32[]{:S(2)}, u32[]{:S(2)}) collective-permute-start(f32[7,128]{1,0:T(8,128)S(1)} %add.265.rest_0_), channel_id=1, source_target_pairs={{0,24},{8,16},{16,8},{24,0},{1,25},{9,17},{17,9},{25,1},{2,26},{10... | collective-permute-start | bytes 10760 | tf_op jit(solution)/shard_map/ppermute | solution.py:350

commit v6 on v5

--- a/solution.py
+++ b/solution.py
@@ -203,20 +203,24 @@
         high = [times_conj(sub(plus[m], minus[m]), rho) for m in range(2)]
         return join(low + high)
 
-    for op in range(FWD_OPS):
-        re, im = column_forward(
-            x_ref[:, op, 0].reshape(rows, LANES), x_ref[:, op, 1].reshape(rows, LANES)
-        )
-        turn_re, turn_im = turn_ref[0], turn_ref[1]
-        turned = jnp.concatenate(
-            [re * turn_re - im * turn_im, re * turn_im + im * turn_re], axis=1
-        )
-        lhs_ref[op] = wide_left(split16(turned))
-
-    copies[0].wait()
-    shape = spec_ref.shape
-    left = lhs_ref[...].reshape(shape[0] * shape[1], lhs_ref.shape[2])
-    spec_ref[...] = dot32(left, b_ref[0]).reshape(shape)
+    def forward(first, last):
+        for op in range(first, last):
+            re, im = column_forward(
+                x_ref[:, op, 0].reshape(rows, LANES), x_ref[:, op, 1].reshape(rows, LANES)
+            )
+            turn_re, turn_im = turn_ref[0], turn_ref[1]
+            turned = jnp.concatenate(
+                [re * turn_re - im * turn_im, re * turn_im + im * turn_re], axis=1
+            )
+            lhs_ref[op] = wide_left(split16(turned))
+        if first == 0:
+            copies[0].wait()
+        count = last - first
+        left = lhs_ref[first:last].reshape(count * rows, lhs_ref.shape[2])
+        spec_ref[first:last] = dot32(left, b_ref[0]).reshape(count, rows, 2 * LANES)
+
+    forward(0, 4)
+    forward(4, FWD_OPS)
 
     totals = sum(ref[...] for ref in totals_refs)
     totals = damp * jnp.sum(totals, axis=1, keepdims=True)
@@ -233,7 +237,7 @@
             im = im + (left_re * right_im + left_im * right_re)
         return re, im
 
-    for out, pairs in enumerate((((2, 1), (0, 3)), ((4, 1), (0, 5), (6, 3)))):
+    def backward(out, pairs):
         re, im = products(pairs)
         re = re + sum(totals[a : a + 1] * totals[b : b + 1] for a, b in pairs)
         h_re, h_im = h_ref[0], h_ref[1]
@@ -246,6 +250,9 @@
         for which, value in enumerate((re, im)):
             piece = (out_ref.shape[0],) + out_ref.shape[3:]
             out_ref[:, out, which] = value.reshape(piece)
+
+    backward(0, ((2, 1), (0, 3)))
+    backward(1, ((4, 1), (0, 5), (6, 3)))
 
 
 def call(kernel, name, out_shapes, *args, near, scratch=()):

time: 124 us -> 124 us (level)
  no operation moved by 1% of the time
where the time goes in v6:
time: 124 us; the launch traced here: 123 us
  blocking collectives  68.5 us (55%)
  waiting for transfers between devices  28.5 us (23%)
  starting transfers between devices  14.5 us (12%)
  Pallas kernels  6.98 us (6%)
  other arithmetic  3.56 us (3%)
    all_to_all x3, blocking collectives, exchange(): return lax.all_to_all(value, AXES, split_axis=0, concat_axis=0, tiled=True)  68.5 us
    ppermute x3, waiting for transfers between devices, group_parts(): lax.ppermute(sums, 'grp', [(d, d ^ step * k) for d in range(count)])  20.8 us
    ppermute x3, waiting for transfers between devices, sum_over_lanes(): lax.ppermute(sums, 'lane', [(d, d ^ step) for d in range(count)])  7.68 us
    pallas_call x5, Pallas kernels, call(): pl.pallas_call(kernel, out_shape=outs, in_specs=specs[:len(args)], out_sp...  6.98 us
    ppermute x3, starting transfers between devices, group_parts(): lax.ppermute(sums, 'grp', [(d, d ^ step * k) for d in range(count)])  6.42 us
    ppermute x3, starting transfers between devices, sum_over_lanes(): lax.ppermute(sums, 'lane', [(d, d ^ step) for d in range(count)])  4.48 us
    all_to_all x1, starting transfers between devices, exchange(): return lax.all_to_all(value, AXES, split_axis=0, concat_axis=0, tiled=True)  3.63 us
  transfers between devices with their start and end apart: 7, of which 5 were waited for; matrix products, arithmetic and copies ran while one was open for 3% of the time, Pallas kernels for 0%

profile of v6, /device:TPU:0, one launch (start us, length us, event | category | flops | bytes accessed | tf_op | source)
XLA Modules:
  0.0 123.2 jit_solution(1575092439695455813)
XLA Ops:
  0.6 1.3 %stack.10 = f32[32,7,8,128]{3,2,1,0:T(8,128)S(1)} custom-call(f32[32,8,128]{2,1,0:T(8,128)} %bitcast.13, f32[32,8,128]{2,1,0:T(8,128)} %bitcast.14, f32[32,8,128]{2,1,0:T(8,128)} %bitcast.15, f32[32,8,128]{2,1,0:T(8,128)} %bitcast.16, f32[32,8,128]{2,1,0:T(8,128)} %bitcast.17, f32[32,8,128]{2,1,0:T(8,128)} %bitcast.18, f32[32,8,128]{2,1,0:T(8,128)} %bitcast.19), custom_call_target="tpu_custom_call" | custom-call | tf_op jit(solution)/shard_map/stack/pallas_call | solution.py:263
  1.9 30.5 %all_to_all.20.x_ref = f32[32,7,8,128]{3,2,1,0:T(8,128)S(1)} all-to-all(f32[32,7,8,128]{3,2,1,0:T(8,128)S(1)} %stack.10), channel_id=1, replica_groups=mesh['grp'=4,'lane'=8] {'grp','lane'}, dimensions={0} | all-to-all | bytes 1835008 | tf_op jit(solution)/shard_map/all_to_all | solution.py:275
  32.5 1.6 %spread.1 = f32[32,7,2,8,128]{4,3,2,1,0:T(8,128)} custom-call(f32[32,7,8,128]{3,2,1,0:T(8,128)S(1)} %all_to_all.20.x_ref), custom_call_target="tpu_custom_call" | custom-call | tf_op jit(solution)/shard_map/spread/pallas_call | solution.py:263
  34.0 3.6 %all-to-all-start.1 = ((f32[32,7,2,8,128]{4,3,2,1,0:T(8,128)}), f32[32,7,2,8,128]{4,3,2,1,0:T(8,128)S(1)}, u32[]{:S(2)}, u32[]{:S(2)}) async-start(f32[32,7,2,8,128]{4,3,2,1,0:T(8,128)} %spread.1), calls=%async_computation.1 | async-start | bytes 3670016 | tf_op jit(solution)/shard_map/all_to_all | solution.py:275
  37.8 1.1 fusion.14
  38.9 0.1 reduce-precision_convert_fusion
  39.0 0.1 multiply_exponential_fusion
  39.1 1.6 %fusion.13 = (f32[1,256,128]{2,1,0:T(8,128)S(1)}, f32[1,256,128]{2,1,0:T(8,128)S(1)}, f32[1,256,128]{2,1,0:T(8,128)S(1)}, f32[1,256,128]{2,1,0:T(8,128)S(1)}) fusion(s32[128]{0:T(128)S(1)} %iota_multiply_fusion.1, s32[]{:T(128)S(6)} %add.239, s32[256]{0:T(256)S(1)} %iota_shift-right-logical_fusion, s32[256]{0:T(256)S(1)} %broadcast_add_fusion, ...), kind=kLoop, calls=%fused_computation.41 | loop fusion | flops 1474560 | bytes 529412 | tf_op jit(solution)/shard_map/mul | solution.py:326
  40.7 0.1 multiply_reduce_fusion
  40.8 0.3 collective-permute-start
  41.2 0.9 collective-permute-done
  42.1 1.8 %collective-permute-start.1 = (f32[7,128]{1,0:T(8,128)S(1)}, f32[7,128]{1,0:T(8,128)S(1)}, u32[]{:S(2)}, u32[]{:S(2)}) collective-permute-start(f32[7,128]{1,0:T(8,128)S(1)} %add.263), channel_id=1, source_target_pairs={{0,2},{1,3},{2,0},{3,1},{4,6},{5,7},{6,4},{7,5},{8,10},{9,11},{10,... | collective-permute-start | bytes 10760 | tf_op jit(solution)/shard_map/ppermute | solution.py:344
  43.8 0.2 pad_maximum_fusion.1.a_ref
  44.0 5.6 %collective-permute-done.1 = f32[7,128]{1,0:T(8,128)S(1)} collective-permute-done((f32[7,128]{1,0:T(8,128)S(1)}, f32[7,128]{1,0:T(8,128)S(1)}, u32[]{:S(2)}, u32[]{:S(2)}) %collective-permute-start.1) | collective-permute-done | bytes 3616 | tf_op jit(solution)/shard_map/ppermute | solution.py:344
  49.6 2.4 %collective-permute-start.2 = (f32[7,128]{1,0:T(8,128)S(1)}, f32[7,128]{1,0:T(8,128)S(1)}, u32[]{:S(2)}, u32[]{:S(2)}) collective-permute-start(f32[7,128]{1,0:T(8,128)S(1)} %add.264), channel_id=1, source_target_pairs={{0,4},{1,5},{2,6},{3,7},{4,0},{5,1},{6,2},{7,3},{8,12},{9,13},{10,... | collective-permute-start | bytes 10760 | tf_op jit(solution)/shard_map/ppermute | solution.py:344
  52.0 0.2 pad_maximum_fusion.3.ai_ref
  52.6 1.2 collective-permute-done.2
  53.8 0.6 collective-permute-start.3
  54.3 5.9 %collective-permute-start.4 = (f32[7,128]{1,0:T(8,128)S(1)}, f32[7,128]{1,0:T(8,128)S(1)}, u32[]{:S(2)}, u32[]{:S(2)}) collective-permute-start(f32[7,128]{1,0:T(8,128)S(1)} %add.265.rest_0_), channel_id=1, source_target_pairs={{0,16},{8,24},{16,0},{24,8},{1,17},{9,25},{17,1},{25,9},{2,18},{10... | collective-permute-start | bytes 10760 | tf_op jit(solution)/shard_map/ppermute | solution.py:357
  60.2 0.0 collective-permute-start.5
  60.2 0.1 maximum_maximum_fusion
  60.3 8.6 %collective-permute-done.3.rest_1_ = f32[7,128]{1,0:T(8,128)S(1)} collective-permute-done((f32[7,128]{1,0:T(8,128)S(1)}, f32[7,128]{1,0:T(8,128)S(1)}, u32[]{:S(2)}, u32[]{:S(2)}) %collective-permute-start.3) | collective-permute-done | bytes 3616 | tf_op jit(solution)/shard_map/ppermute | solution.py:357
  68.8 12.2 %collective-permute-done.4.rest_2_ = f32[7,128]{1,0:T(8,128)S(1)} collective-permute-done((f32[7,128]{1,0:T(8,128)S(1)}, f32[7,128]{1,0:T(8,128)S(1)}, u32[]{:S(2)}, u32[]{:S(2)}) %collective-permute-start.4) | collective-permute-done | bytes 3616 | tf_op jit(solution)/shard_map/ppermute | solution.py:357
  81.1 0.0 collective-permute-done.5.rest_3_
  81.1 0.0 all-to-all-done.1.x_ref
  81.1 0.1 broadcast.940.roots_ref
  81.1 3.1 %spectrum.1 = f32[32,2,2,8,128]{4,3,2,1,0:T(8,128)S(1)} custom-call(f32[32,7,2,8,128]{4,3,2,1,0:T(8,128)S(1)} %all-to-all-done.1.x_ref, bf16[4,128,256]{2,1,0:T(8,128)(2,1)S(1)} %pad_maximum_fusion.1.a_ref, bf16[4,128,256]{2,1,0:T(8,128)(2,1)S(1)} %pad_maximum_fusion.3.ai_ref, f32[2,256,128]{2,1,0:T(8,128)S(1)} %get-tuple-element.20.turn_ref, ...), custom_call_target="tpu_custom_call" | custom-call | tf_op jit(solution)/shard_map/spectrum/pallas_call | solution.py:263
  84.2 19.5 %all_to_all.21.u_ref = f32[32,2,2,8,128]{4,3,2,1,0:T(8,128)S(1)} all-to-all(f32[32,2,2,8,128]{4,3,2,1,0:T(8,128)S(1)} %spectrum.1), channel_id=1, replica_groups=mesh['grp'=4,'lane'=8] {'grp','lane'}, dimensions={0} | all-to-all | bytes 1048576 | tf_op jit(solution)/shard_map/all_to_all | solution.py:275
  103.8 0.2 gather.1
  104.0 18.4 %all_to_all.22.in_ref = f32[32,2,2,8,128]{4,3,2,1,0:T(8,128)S(1)} all-to-all(f32[32,2,2,8,128]{4,3,2,1,0:T(8,128)S(1)} %gather.1), channel_id=1, replica_groups=mesh['grp'=4,'lane'=8] {'grp','lane'}, dimensions={0} | all-to-all | bytes 1048576 | tf_op jit(solution)/shard_map/all_to_all | solution.py:275
  122.4 0.8 deliver.1
  (14 shorter events, 0.1 us)
Async XLA Ops:
  34.0 47.0 %all-to-all-start.1 = ((f32[32,7,2,8,128]{4,3,2,1,0:T(8,128)}), f32[32,7,2,8,128]{4,3,2,1,0:T(8,128)S(1)}, u32[]{:S(2)}, u32[]{:S(2)}) async-start(f32[32,7,2,8,128]{4,3,2,1,0:T(8,128)} %spread.1), calls=%async_computation.1 | async-start | bytes 3670016 | tf_op jit(solution)/shard_map/all_to_all | solution.py:275
  40.8 1.2 collective-permute-start
  42.1 7.6 %collective-permute-start.1 = (f32[7,128]{1,0:T(8,128)S(1)}, f32[7,128]{1,0:T(8,128)S(1)}, u32[]{:S(2)}, u32[]{:S(2)}) collective-permute-start(f32[7,128]{1,0:T(8,128)S(1)} %add.263), channel_id=1, source_target_pairs={{0,2},{1,3},{2,0},{3,1},{4,6},{5,7},{6,4},{7,5},{8,10},{9,11},{10,... | collective-permute-start | bytes 10760 | tf_op jit(solution)/shard_map/ppermute | solution.py:344
  49.6 4.1 %collective-permute-start.2 = (f32[7,128]{1,0:T(8,128)S(1)}, f32[7,128]{1,0:T(8,128)S(1)}, u32[]{:S(2)}, u32[]{:S(2)}) collective-permute-start(f32[7,128]{1,0:T(8,128)S(1)} %add.264), channel_id=1, source_target_pairs={{0,4},{1,5},{2,6},{3,7},{4,0},{5,1},{6,2},{7,3},{8,12},{9,13},{10,... | collective-permute-start | bytes 10760 | tf_op jit(solution)/shard_map/ppermute | solution.py:344
  53.8 15.1 %collective-permute-start.3 = (f32[7,128]{1,0:T(8,128)S(1)}, f32[7,128]{1,0:T(8,128)S(1)}, u32[]{:S(2)}, u32[]{:S(2)}) collective-permute-start(f32[7,128]{1,0:T(8,128)S(1)} %add.265.rest_0_), channel_id=1, source_target_pairs={{0,8},{8,0},{16,24},{24,16},{1,9},{9,1},{17,25},{25,17},{2,10},{10... | collective-permute-start | bytes 10760 | tf_op jit(solution)/shard_map/ppermute | solution.py:357
  54.3 26.7 %collective-permute-start.4 = (f32[7,128]{1,0:T(8,128)S(1)}, f32[7,128]{1,0:T(8,128)S(1)}, u32[]{:S(2)}, u32[]{:S(2)}) collective-permute-start(f32[7,128]{1,0:T(8,128)S(1)} %add.265.rest_0_), channel_id=1, source_target_pairs={{0,16},{8,24},{16,0},{24,8},{1,17},{9,25},{17,1},{25,9},{2,18},{10... | collective-permute-start | bytes 10760 | tf_op jit(solution)/shard_map/ppermute | solution.py:357
  60.2 20.9 %collective-permute-start.5 = (f32[7,128]{1,0:T(8,128)S(1)}, f32[7,128]{1,0:T(8,128)S(1)}, u32[]{:S(2)}, u32[]{:S(2)}) collective-permute-start(f32[7,128]{1,0:T(8,128)S(1)} %add.265.rest_0_), channel_id=1, source_target_pairs={{0,24},{8,16},{16,8},{24,0},{1,25},{9,17},{17,9},{25,1},{2,26},{10... | collective-permute-start | bytes 10760 | tf_op jit(solution)/shard_map/ppermute | solution.py:357

commit v7 on v6

--- a/solution.py
+++ b/solution.py
@@ -237,22 +237,19 @@
             im = im + (left_re * right_im + left_im * right_re)
         return re, im
 
-    def backward(out, pairs):
+    damped = []
+    for pairs in (((2, 1), (0, 3)), ((4, 1), (0, 5), (6, 3))):
         re, im = products(pairs)
         re = re + sum(totals[a : a + 1] * totals[b : b + 1] for a, b in pairs)
-        h_re, h_im = h_ref[0], h_ref[1]
-        damped = jnp.concatenate([re * h_re - im * h_im, re * h_im + im * h_re], axis=1)
-        both = dot32(wide_left(split16(damped)), b_ref[1])
-        re, im = both[:, :LANES], both[:, LANES:]
-        turn_re, turn_im = turn_ref[0], turn_ref[1]
-        re, im = re * turn_re + im * turn_im, im * turn_re - re * turn_im
-        re, im = column_inverse(re, im)
-        for which, value in enumerate((re, im)):
+        value = times((re, im), (h_ref[0], h_ref[1]))
+        damped.append(wide_left(split16(jnp.concatenate(value, axis=1))))
+    both = dot32(jnp.concatenate(damped, axis=0), b_ref[1])
+    for out in range(2):
+        part = both[out * rows : (out + 1) * rows]
+        value = times_conj((part[:, :LANES], part[:, LANES:]), (turn_ref[0], turn_ref[1]))
+        for which, value in enumerate(column_inverse(*value)):
             piece = (out_ref.shape[0],) + out_ref.shape[3:]
             out_ref[:, out, which] = value.reshape(piece)
-
-    backward(0, ((2, 1), (0, 3)))
-    backward(1, ((4, 1), (0, 5), (6, 3)))
 
 
 def call(kernel, name, out_shapes, *args, near, scratch=()):

time: 124 us -> 124 us (level)
  no operation moved by 1% of the time
where the time goes in v7:
time: 124 us; the launch traced here: 123 us
  blocking collectives  68.5 us (55%)
  waiting for transfers between devices  28.5 us (23%)
  starting transfers between devices  14.5 us (12%)
  Pallas kernels  6.99 us (6%)
  other arithmetic  3.56 us (3%)
    all_to_all x3, blocking collectives, exchange(): return lax.all_to_all(value, AXES, split_axis=0, concat_axis=0, tiled=True)  68.5 us
    ppermute x3, waiting for transfers between devices, group_parts(): lax.ppermute(sums, 'grp', [(d, d ^ step * k) for d in range(count)])  20.8 us
    ppermute x3, waiting for transfers between devices, sum_over_lanes(): lax.ppermute(sums, 'lane', [(d, d ^ step) for d in range(count)])  7.68 us
    pallas_call x5, Pallas kernels, call(): pl.pallas_call(kernel, out_shape=outs, in_specs=specs[:len(args)], out_sp...  6.99 us
    ppermute x3, starting transfers between devices, group_parts(): lax.ppermute(sums, 'grp', [(d, d ^ step * k) for d in range(count)])  6.42 us
    ppermute x3, starting transfers between devices, sum_over_lanes(): lax.ppermute(sums, 'lane', [(d, d ^ step) for d in range(count)])  4.48 us
    all_to_all x1, starting transfers between devices, exchange(): return lax.all_to_all(value, AXES, split_axis=0, concat_axis=0, tiled=True)  3.63 us
  transfers between devices with their start and end apart: 7, of which 5 were waited for; matrix products, arithmetic and copies ran while one was open for 3% of the time, Pallas kernels for 0%

profile of v7, /device:TPU:0, one launch (start us, length us, event | category | flops | bytes accessed | tf_op | source)
XLA Modules:
  0.0 123.2 jit_solution(11262336038070743210)
XLA Ops:
  0.6 1.3 %stack.10 = f32[32,7,8,128]{3,2,1,0:T(8,128)S(1)} custom-call(f32[32,8,128]{2,1,0:T(8,128)} %bitcast.13, f32[32,8,128]{2,1,0:T(8,128)} %bitcast.14, f32[32,8,128]{2,1,0:T(8,128)} %bitcast.15, f32[32,8,128]{2,1,0:T(8,128)} %bitcast.16, f32[32,8,128]{2,1,0:T(8,128)} %bitcast.17, f32[32,8,128]{2,1,0:T(8,128)} %bitcast.18, f32[32,8,128]{2,1,0:T(8,128)} %bitcast.19), custom_call_target="tpu_custom_call" | custom-call | tf_op jit(solution)/shard_map/stack/pallas_call | solution.py:260
  1.9 30.5 %all_to_all.20.x_ref = f32[32,7,8,128]{3,2,1,0:T(8,128)S(1)} all-to-all(f32[32,7,8,128]{3,2,1,0:T(8,128)S(1)} %stack.10), channel_id=1, replica_groups=mesh['grp'=4,'lane'=8] {'grp','lane'}, dimensions={0} | all-to-all | bytes 1835008 | tf_op jit(solution)/shard_map/all_to_all | solution.py:272
  32.5 1.6 %spread.1 = f32[32,7,2,8,128]{4,3,2,1,0:T(8,128)} custom-call(f32[32,7,8,128]{3,2,1,0:T(8,128)S(1)} %all_to_all.20.x_ref), custom_call_target="tpu_custom_call" | custom-call | tf_op jit(solution)/shard_map/spread/pallas_call | solution.py:260
  34.0 3.6 %all-to-all-start.1 = ((f32[32,7,2,8,128]{4,3,2,1,0:T(8,128)}), f32[32,7,2,8,128]{4,3,2,1,0:T(8,128)S(1)}, u32[]{:S(2)}, u32[]{:S(2)}) async-start(f32[32,7,2,8,128]{4,3,2,1,0:T(8,128)} %spread.1), calls=%async_computation.1 | async-start | bytes 3670016 | tf_op jit(solution)/shard_map/all_to_all | solution.py:272
  37.8 1.1 fusion.14
  38.9 0.1 reduce-precision_convert_fusion
  39.0 0.1 multiply_exponential_fusion
  39.1 1.6 %fusion.13 = (f32[1,256,128]{2,1,0:T(8,128)S(1)}, f32[1,256,128]{2,1,0:T(8,128)S(1)}, f32[1,256,128]{2,1,0:T(8,128)S(1)}, f32[1,256,128]{2,1,0:T(8,128)S(1)}) fusion(s32[128]{0:T(128)S(1)} %iota_multiply_fusion.1, s32[]{:T(128)S(6)} %add.239, s32[256]{0:T(256)S(1)} %iota_shift-right-logical_fusion, s32[256]{0:T(256)S(1)} %broadcast_add_fusion, ...), kind=kLoop, calls=%fused_computation.41 | loop fusion | flops 1474560 | bytes 529412 | tf_op jit(solution)/shard_map/mul | solution.py:323
  40.7 0.1 multiply_reduce_fusion
  40.8 0.3 collective-permute-start
  41.2 0.9 collective-permute-done
  42.1 1.8 %collective-permute-start.1 = (f32[7,128]{1,0:T(8,128)S(1)}, f32[7,128]{1,0:T(8,128)S(1)}, u32[]{:S(2)}, u32[]{:S(2)}) collective-permute-start(f32[7,128]{1,0:T(8,128)S(1)} %add.263), channel_id=1, source_target_pairs={{0,2},{1,3},{2,0},{3,1},{4,6},{5,7},{6,4},{7,5},{8,10},{9,11},{10,... | collective-permute-start | bytes 10760 | tf_op jit(solution)/shard_map/ppermute | solution.py:341
  43.8 0.2 pad_maximum_fusion.1.a_ref
  44.0 5.6 %collective-permute-done.1 = f32[7,128]{1,0:T(8,128)S(1)} collective-permute-done((f32[7,128]{1,0:T(8,128)S(1)}, f32[7,128]{1,0:T(8,128)S(1)}, u32[]{:S(2)}, u32[]{:S(2)}) %collective-permute-start.1) | collective-permute-done | bytes 3616 | tf_op jit(solution)/shard_map/ppermute | solution.py:341
  49.6 2.4 %collective-permute-start.2 = (f32[7,128]{1,0:T(8,128)S(1)}, f32[7,128]{1,0:T(8,128)S(1)}, u32[]{:S(2)}, u32[]{:S(2)}) collective-permute-start(f32[7,128]{1,0:T(8,128)S(1)} %add.264), channel_id=1, source_target_pairs={{0,4},{1,5},{2,6},{3,7},{4,0},{5,1},{6,2},{7,3},{8,12},{9,13},{10,... | collective-permute-start | bytes 10760 | tf_op jit(solution)/shard_map/ppermute | solution.py:341
  52.0 0.2 pad_maximum_fusion.3.ai_ref
  52.6 1.2 collective-permute-done.2
  53.8 0.6 collective-permute-start.3
  54.3 5.9 %collective-permute-start.4 = (f32[7,128]{1,0:T(8,128)S(1)}, f32[7,128]{1,0:T(8,128)S(1)}, u32[]{:S(2)}, u32[]{:S(2)}) collective-permute-start(f32[7,128]{1,0:T(8,128)S(1)} %add.265.rest_0_), channel_id=1, source_target_pairs={{0,16},{8,24},{16,0},{24,8},{1,17},{9,25},{17,1},{25,9},{2,18},{10... | collective-permute-start | bytes 10760 | tf_op jit(solution)/shard_map/ppermute | solution.py:354
  60.2 0.0 collective-permute-start.5
  60.2 0.1 maximum_maximum_fusion
  60.3 8.6 %collective-permute-done.3.rest_1_ = f32[7,128]{1,0:T(8,128)S(1)} collective-permute-done((f32[7,128]{1,0:T(8,128)S(1)}, f32[7,128]{1,0:T(8,128)S(1)}, u32[]{:S(2)}, u32[]{:S(2)}) %collective-permute-start.3) | collective-permute-done | bytes 3616 | tf_op jit(solution)/shard_map/ppermute | solution.py:354
  68.8 12.2 %collective-permute-done.4.rest_2_ = f32[7,128]{1,0:T(8,128)S(1)} collective-permute-done((f32[7,128]{1,0:T(8,128)S(1)}, f32[7,128]{1,0:T(8,128)S(1)}, u32[]{:S(2)}, u32[]{:S(2)}) %collective-permute-start.4) | collective-permute-done | bytes 3616 | tf_op jit(solution)/shard_map/ppermute | solution.py:354
  81.1 0.0 collective-permute-done.5.rest_3_
  81.1 0.0 all-to-all-done.1.x_ref
  81.1 0.1 broadcast.940.roots_ref
  81.1 3.1 %spectrum.1 = f32[32,2,2,8,128]{4,3,2,1,0:T(8,128)S(1)} custom-call(f32[32,7,2,8,128]{4,3,2,1,0:T(8,128)S(1)} %all-to-all-done.1.x_ref, bf16[4,128,256]{2,1,0:T(8,128)(2,1)S(1)} %pad_maximum_fusion.1.a_ref, bf16[4,128,256]{2,1,0:T(8,128)(2,1)S(1)} %pad_maximum_fusion.3.ai_ref, f32[2,256,128]{2,1,0:T(8,128)S(1)} %get-tuple-element.20.turn_ref, ...), custom_call_target="tpu_custom_call" | custom-call | tf_op jit(solution)/shard_map/spectrum/pallas_call | solution.py:260
  84.2 19.5 %all_to_all.21.u_ref = f32[32,2,2,8,128]{4,3,2,1,0:T(8,128)S(1)} all-to-all(f32[32,2,2,8,128]{4,3,2,1,0:T(8,128)S(1)} %spectrum.1), channel_id=1, replica_groups=mesh['grp'=4,'lane'=8] {'grp','lane'}, dimensions={0} | all-to-all | bytes 1048576 | tf_op jit(solution)/shard_map/all_to_all | solution.py:272
  103.8 0.2 gather.1
  104.0 18.4 %all_to_all.22.in_ref = f32[32,2,2,8,128]{4,3,2,1,0:T(8,128)S(1)} all-to-all(f32[32,2,2,8,128]{4,3,2,1,0:T(8,128)S(1)} %gather.1), channel_id=1, replica_groups=mesh['grp'=4,'lane'=8] {'grp','lane'}, dimensions={0} | all-to-all | bytes 1048576 | tf_op jit(solution)/shard_map/all_to_all | solution.py:272
  122.4 0.8 deliver.1
  (14 shorter events, 0.1 us)
Async XLA Ops:
  34.0 47.0 %all-to-all-start.1 = ((f32[32,7,2,8,128]{4,3,2,1,0:T(8,128)}), f32[32,7,2,8,128]{4,3,2,1,0:T(8,128)S(1)}, u32[]{:S(2)}, u32[]{:S(2)}) async-start(f32[32,7,2,8,128]{4,3,2,1,0:T(8,128)} %spread.1), calls=%async_computation.1 | async-start | bytes 3670016 | tf_op jit(solution)/shard_map/all_to_all | solution.py:272
  40.8 1.2 collective-permute-start
  42.1 7.6 %collective-permute-start.1 = (f32[7,128]{1,0:T(8,128)S(1)}, f32[7,128]{1,0:T(8,128)S(1)}, u32[]{:S(2)}, u32[]{:S(2)}) collective-permute-start(f32[7,128]{1,0:T(8,128)S(1)} %add.263), channel_id=1, source_target_pairs={{0,2},{1,3},{2,0},{3,1},{4,6},{5,7},{6,4},{7,5},{8,10},{9,11},{10,... | collective-permute-start | bytes 10760 | tf_op jit(solution)/shard_map/ppermute | solution.py:341
  49.6 4.1 %collective-permute-start.2 = (f32[7,128]{1,0:T(8,128)S(1)}, f32[7,128]{1,0:T(8,128)S(1)}, u32[]{:S(2)}, u32[]{:S(2)}) collective-permute-start(f32[7,128]{1,0:T(8,128)S(1)} %add.264), channel_id=1, source_target_pairs={{0,4},{1,5},{2,6},{3,7},{4,0},{5,1},{6,2},{7,3},{8,12},{9,13},{10,... | collective-permute-start | bytes 10760 | tf_op jit(solution)/shard_map/ppermute | solution.py:341
  53.8 15.1 %collective-permute-start.3 = (f32[7,128]{1,0:T(8,128)S(1)}, f32[7,128]{1,0:T(8,128)S(1)}, u32[]{:S(2)}, u32[]{:S(2)}) collective-permute-start(f32[7,128]{1,0:T(8,128)S(1)} %add.265.rest_0_), channel_id=1, source_target_pairs={{0,8},{8,0},{16,24},{24,16},{1,9},{9,1},{17,25},{25,17},{2,10},{10... | collective-permute-start | bytes 10760 | tf_op jit(solution)/shard_map/ppermute | solution.py:354
  54.3 26.7 %collective-permute-start.4 = (f32[7,128]{1,0:T(8,128)S(1)}, f32[7,128]{1,0:T(8,128)S(1)}, u32[]{:S(2)}, u32[]{:S(2)}) collective-permute-start(f32[7,128]{1,0:T(8,128)S(1)} %add.265.rest_0_), channel_id=1, source_target_pairs={{0,16},{8,24},{16,0},{24,8},{1,17},{9,25},{17,1},{25,9},{2,18},{10... | collective-permute-start | bytes 10760 | tf_op jit(solution)/shard_map/ppermute | solution.py:354
  60.2 20.9 %collective-permute-start.5 = (f32[7,128]{1,0:T(8,128)S(1)}, f32[7,128]{1,0:T(8,128)S(1)}, u32[]{:S(2)}, u32[]{:S(2)}) collective-permute-start(f32[7,128]{1,0:T(8,128)S(1)} %add.265.rest_0_), channel_id=1, source_target_pairs={{0,24},{8,16},{16,8},{24,0},{1,25},{9,17},{17,9},{25,1},{2,26},{10... | collective-permute-start | bytes 10760 | tf_op jit(solution)/shard_map/ppermute | solution.py:354
